TPU v7x, 32 devices: a whole 2x2x4 slice. The times are simulated.
32 devices in a mesh: aa: 8 (over y, x, core), ba: 4 (over z).
Axes of the slice: x: 2, y: 2, z: 4, core: 2. Of those that a mesh axis runs over, the one named last changes fastest.
Arguments:
- query: bfloat16 [3072, 4096], P('aa', 'ba'), may hold values from -28 to 28
- keys: bfloat16 [3072, 2048], P('aa', 'ba'), may hold values from -6 to 6
- values: bfloat16 [3072, 2048], P('aa', 'ba'), may hold values from -6 to 6
- grad_out: bfloat16 [3072, 5376], P('aa', 'ba'), may hold values from -6 to 6
- segment_ids: int32 [3072], P('aa'), may hold values from 0 to 5, never falling along the last dimension, each value on 1 to 1920 neighbouring positions
- w_query: bfloat16 [5376, 4096], P(None, 'ba'), may hold values from -0.125 to 0.125
- w_key: bfloat16 [5376, 2048], P(None, 'ba'), may hold values from -0.1875 to 0.1875
- w_value: bfloat16 [5376, 2048], P(None, 'ba'), may hold values from -0.1875 to 0.1875
- w_out: bfloat16 [4096, 5376], P('ba'), may hold values from -0.078125 to 0.078125
Outputs:
- grad_input: bfloat16 [3072, 5376], P('aa', 'ba')
Inputs may be any that keep to these rules, and one draw needn't show every extreme that they name: `segment_ids`: never falls along the sequence; each document has at most 1920 positions.
All inputs are finite; a program needn't handle non-finite values.
Results may differ from a plain program's by a relative error of at most 0.019.
Values may be sent and summed in bfloat16 or wider, within the bound.
A program may use at most 128 MiB of HBM per device.

v0:
```python
import functools

import jax
import jax.numpy as jnp
from jax import lax
from jax.experimental import pallas as pl
from jax.experimental.pallas import tpu as pltpu
from jax.sharding import PartitionSpec as P

D = 5376
HQ = 32
HD = 128
DOCS = 6


NEG_FILL = -1e30


def from_behind(value, axis, steps):
    count = lax.axis_size(axis)
    pairs = [(source, (source + steps) % count) for source in range(count)]
    return lax.ppermute(value, axis, pairs)


def block_scores(query, dout, keys, values, query_pos, query_seg, key_pos, key_seg, scaling):
    row_count = query.shape[0]
    col_count = keys.shape[0]
    groups = keys.shape[1] // HD
    query_four = query.reshape(row_count, groups, 2, HD)
    dout_four = dout.reshape(row_count, groups, 2, HD)
    key_three = keys.reshape(col_count, groups, HD)
    value_three = values.reshape(col_count, groups, HD)
    scores = (
        jnp.einsum("iagd,jad->agij", query_four, key_three, preferred_element_type=jnp.float32)
        * scaling
    )
    dprobs = jnp.einsum(
        "iagd,jad->agij", dout_four, value_three, preferred_element_type=jnp.float32
    )
    allowed = (key_pos[None, :] <= query_pos[:, None]) & (key_seg[None, :] == query_seg[:, None])
    return (scores, dprobs, allowed, query_four, dout_four, key_three)


def forward_stats(
    query, dout, keys, values, query_pos, query_seg, key_pos, key_seg, scaling, state
):
    run_max, run_sum, run_dot = state
    scores, dprobs, allowed, unused_q, unused_d, unused_k = block_scores(
        query, dout, keys, values, query_pos, query_seg, key_pos, key_seg, scaling
    )
    masked = jnp.where(allowed, scores, NEG_FILL)
    new_max = jnp.maximum(run_max, jnp.max(masked, axis=-1))
    expo = jnp.where(allowed, jnp.exp(scores - new_max[..., None]), 0.0)
    return (new_max, jnp.sum(expo, axis=-1), jnp.sum(expo * dprobs, axis=-1))


def block_grads(
    query, dout, row_lse, row_delta, keys, values, query_pos, query_seg, key_pos, key_seg, scaling
):
    scores, dprobs, allowed, query_four, dout_four, key_three = block_scores(
        query, dout, keys, values, query_pos, query_seg, key_pos, key_seg, scaling
    )
    softmax_w = jnp.where(allowed, jnp.exp(scores - row_lse[..., None]), 0.0)
    dscores = softmax_w * (dprobs - row_delta[..., None])
    softmax_low = softmax_w.astype(jnp.bfloat16)
    dscores_low = dscores.astype(jnp.bfloat16)
    grad_v = jnp.einsum(
        "agij,iagd->jad", softmax_low, dout_four, preferred_element_type=jnp.float32
    )
    grad_k = (
        jnp.einsum("agij,iagd->jad", dscores_low, query_four, preferred_element_type=jnp.float32)
        * scaling
    )
    grad_q = (
        jnp.einsum("agij,jad->iagd", dscores_low, key_three, preferred_element_type=jnp.float32)
        * scaling
    )
    return (
        grad_q.reshape(query.shape[0], -1),
        grad_k.reshape(keys.shape[0], -1),
        grad_v.reshape(keys.shape[0], -1),
    )


def project_back(grad, weight):
    return lax.dot_general(
        grad, weight, (((1,), (1,)), ((), ())), preferred_element_type=jnp.float32
    )


def local_ring(query, keys, values, grad_out, segment_ids, w_query, w_key, w_value, w_out):
    seq_devices = lax.axis_size("aa")
    own_index = lax.axis_index("aa")
    tok_count = query.shape[0]
    scaling = (D / HQ) ** (-0.5)
    groups = keys.shape[1] // HD
    all_seg = lax.all_gather(segment_ids, "aa", axis=0, tiled=True)
    dout = project_back(lax.all_gather(grad_out, "ba", axis=1, tiled=True), w_out).astype(
        jnp.bfloat16
    )
    offsets = lax.iota(jnp.int32, tok_count)
    own_pos = own_index * tok_count + offsets
    own_seg = lax.dynamic_slice_in_dim(all_seg, own_index * tok_count, tok_count)
    stat_shape = (groups, 2, tok_count)
    stats_start = (
        jnp.full(stat_shape, NEG_FILL, jnp.float32),
        jnp.zeros(stat_shape, jnp.float32),
        jnp.zeros(stat_shape, jnp.float32),
    )
    piece = (
        lax.all_gather(keys, "aa", axis=0, tiled=True),
        lax.all_gather(values, "aa", axis=0, tiled=True),
    )
    width = piece[0].shape[0]
    key_pos = lax.iota(jnp.int32, width)
    key_seg = all_seg
    run_max, run_sum, run_dot = forward_stats(
        query, dout, piece[0], piece[1], own_pos, own_seg, key_pos, key_seg, scaling, stats_start
    )
    row_lse = run_max + jnp.log(run_sum)
    row_delta = run_dot / run_sum
    zero_q = jnp.zeros(query.shape, jnp.float32)
    zero_k = jnp.zeros(keys.shape, jnp.float32)

    def step_keys(step_index, state):
        (keys_now, values_now), (dk_now, dv_now), grad_q = state
        anchor = (own_index - step_index) % seq_devices
        key_pos = anchor * tok_count + offsets
        key_seg = lax.dynamic_slice_in_dim(all_seg, anchor * tok_count, tok_count)
        add_q, add_k, add_v = block_grads(
            query,
            dout,
            row_lse,
            row_delta,
            keys_now,
            values_now,
            own_pos,
            own_seg,
            key_pos,
            key_seg,
            scaling,
        )
        bundle_next = from_behind((keys_now, values_now), "aa", 1)
        sums_next = (
            from_behind((dk_now + add_k).astype(jnp.bfloat16), "aa", 1).astype(jnp.float32),
            from_behind((dv_now + add_v).astype(jnp.bfloat16), "aa", 1).astype(jnp.float32),
        )
        return (bundle_next, sums_next, grad_q + add_q)

    initial = ((keys, values), (zero_k, zero_k), zero_q)
    final = lax.fori_loop(0, seq_devices, step_keys, initial)
    grad_q = final[2]
    grad_k = final[1][0]
    grad_v = final[1][1]
    partial_value = (
        project_back(grad_q.astype(jnp.bfloat16), w_query)
        + project_back(grad_k.astype(jnp.bfloat16), w_key)
        + project_back(grad_v.astype(jnp.bfloat16), w_value)
    )
    return lax.psum_scatter(
        partial_value.astype(jnp.bfloat16), "ba", scatter_dimension=1, tiled=True
    )


def fold_rows(value, op):
    return op(value.reshape(-1, 8, value.shape[1]), axis=0)


CONTRACT_LAST = (((1,), (1,)), ((), ()))


def block_of(ref, kb, block, lanes):
    return ref[pl.ds(pl.multiple_of(kb * block, block), block), lanes]


def masked_scores(qkv_ref, query, qb, kb, block, starts, scaling):
    lane = lax.broadcasted_iota(jnp.int32, (block, block), 1)
    sub = lax.broadcasted_iota(jnp.int32, (block, block), 0)
    key = block_of(qkv_ref, kb, block, slice(HD, 2 * HD))
    s = lax.dot_general(key, query, CONTRACT_LAST, preferred_element_type=jnp.float32)
    key_pos = kb * block + sub
    allowed = (key_pos <= qb * block + lane) & (key_pos >= starts)
    return jnp.where(allowed, s * scaling, NEG_FILL)


def stats_kernel(block, scaling, low_ref, start_ref, qkv_ref, lse_ref, s_ref):
    def query_block(qb, carry):
        query = block_of(qkv_ref, qb, block, slice(0, HD))
        low = low_ref[qb]
        starts = start_ref[pl.ds(qb, 1), :]

        def scores_at(kb, top):
            s = masked_scores(qkv_ref, query, qb, kb, block, starts, scaling)
            s_ref[pl.ds(pl.multiple_of(kb * block, block), block), :] = s
            return jnp.maximum(top, fold_rows(s, jnp.max))

        top = lax.fori_loop(low, qb + 1, scores_at, jnp.full((8, block), NEG_FILL, jnp.float32))
        top = jnp.max(top, axis=0, keepdims=True)

        def sums_at(kb, run_sum):
            return run_sum + fold_rows(jnp.exp(block_of(s_ref, kb, block, slice(None)) - top), jnp.sum)

        run_sum = lax.fori_loop(low, qb + 1, sums_at, jnp.zeros((8, block), jnp.float32))
        lse_ref[pl.ds(qb, 1), :] = top + jnp.log(jnp.sum(run_sum, axis=0, keepdims=True))
        return carry

    lax.fori_loop(0, qkv_ref.shape[0] // block, query_block, 0)


def grads_kernel(block, scaling, low_ref, start_ref, lse_ref, qkv_ref, dout_ref, gq_ref, gkv_ref, p_ref, dp_ref, dk_ref, dv_ref):
    dk_ref[...] = jnp.zeros_like(dk_ref)
    dv_ref[...] = jnp.zeros_like(dv_ref)

    def query_block(qb, carry):
        rows = pl.ds(pl.multiple_of(qb * block, block), block)
        query = qkv_ref[rows, 0:HD]
        dout = dout_ref[rows, :]
        low = low_ref[qb]
        starts = start_ref[pl.ds(qb, 1), :]
        lse = lse_ref[pl.ds(qb, 1), :]

        def probs_at(kb, run_dot):
            cols = pl.ds(pl.multiple_of(kb * block, block), block)
            s = masked_scores(qkv_ref, query, qb, kb, block, starts, scaling)
            value = qkv_ref[cols, 2 * HD : 3 * HD]
            dp = lax.dot_general(value, dout, CONTRACT_LAST, preferred_element_type=jnp.float32)
            probs = jnp.exp(s - lse)
            p_ref[cols, :] = probs
            dp_ref[cols, :] = dp
            return run_dot + fold_rows(probs * dp, jnp.sum)

        run_dot = lax.fori_loop(low, qb + 1, probs_at, jnp.zeros((8, block), jnp.float32))
        delta = jnp.sum(run_dot, axis=0, keepdims=True)

        def grads_at(kb, grad_q):
            cols = pl.ds(pl.multiple_of(kb * block, block), block)
            probs = p_ref[cols, :]
            dscores = (probs * (dp_ref[cols, :] - delta)).astype(jnp.bfloat16)
            dv_ref[cols, :] += jnp.dot(probs.astype(jnp.bfloat16), dout, preferred_element_type=jnp.float32)
            dk_ref[cols, :] += jnp.dot(dscores, query, preferred_element_type=jnp.float32)
            return grad_q + lax.dot_general(
                dscores, qkv_ref[cols, HD : 2 * HD], (((0,), (0,)), ((), ())), preferred_element_type=jnp.float32
            )

        grad_q = lax.fori_loop(low, qb + 1, grads_at, jnp.zeros((block, HD), jnp.float32))
        gq_ref[rows, :] = (grad_q * scaling).astype(jnp.bfloat16)
        return carry

    lax.fori_loop(0, qkv_ref.shape[0] // block, query_block, 0)
    gkv_ref[:, 0:HD] = (dk_ref[...] * scaling).astype(jnp.bfloat16)
    gkv_ref[:, HD : 2 * HD] = dv_ref[...].astype(jnp.bfloat16)


def document_starts(all_seg, block):
    chosen = all_seg[None, :] == lax.iota(jnp.int32, DOCS)[:, None]
    firsts = jnp.sum(all_seg[None, :] < lax.iota(jnp.int32, DOCS)[:, None], axis=1, dtype=jnp.int32)
    starts = jnp.sum(jnp.where(chosen, firsts[:, None], 0), axis=0, dtype=jnp.int32).reshape(-1, block)
    return starts[:, 0] // block, starts


WHOLE = pl.BlockSpec(memory_space=pltpu.VMEM)
SCALARS = pl.BlockSpec(memory_space=pltpu.SMEM)


def head_stats(low, starts, qkv, scaling):
    total, block = qkv.shape[0], starts.shape[1]
    return pl.pallas_call(
        functools.partial(stats_kernel, block, scaling),
        out_shape=jax.ShapeDtypeStruct(starts.shape, jnp.float32),
        in_specs=[SCALARS, WHOLE, WHOLE],
        out_specs=WHOLE,
        scratch_shapes=[pltpu.VMEM((total, block), jnp.float32)],
        compiler_params=pltpu.CompilerParams(vmem_limit_bytes=16 * 1024 * 1024),
        cost_estimate=pl.CostEstimate(flops=total * total * HD, bytes_accessed=qkv.size * 2, transcendentals=total * total // 2),
        name="stats",
    )(low, starts, qkv)


def head_grads(low, starts, lse, qkv, dout, scaling):
    total, block = qkv.shape[0], starts.shape[1]
    return pl.pallas_call(
        functools.partial(grads_kernel, block, scaling),
        out_shape=[
            jax.ShapeDtypeStruct((total, HD), jnp.bfloat16),
            jax.ShapeDtypeStruct((total, 2 * HD), jnp.bfloat16),
        ],
        in_specs=[SCALARS, WHOLE, WHOLE, WHOLE, WHOLE],
        out_specs=[WHOLE, WHOLE],
        scratch_shapes=[
            pltpu.VMEM((total, block), jnp.float32),
            pltpu.VMEM((total, block), jnp.float32),
            pltpu.VMEM((total, HD), jnp.float32),
            pltpu.VMEM((total, HD), jnp.float32),
        ],
        compiler_params=pltpu.CompilerParams(vmem_limit_bytes=32 * 1024 * 1024),
        cost_estimate=pl.CostEstimate(flops=5 * total * total * HD, bytes_accessed=qkv.size * 6, transcendentals=total * total // 2),
        name="grads",
    )(low, starts, lse, qkv, dout)


def local(query, keys, values, grad_out, segment_ids, w_query, w_key, w_value, w_out):
    seq_devices = lax.axis_size("aa")
    tok_count = query.shape[0]
    heads = query.shape[1] // HD
    groups = keys.shape[1] // HD
    if heads != seq_devices:
        return local_ring(query, keys, values, grad_out, segment_ids, w_query, w_key, w_value, w_out)
    scaling = (D / HQ) ** (-0.5)
    block = 256 if (tok_count * seq_devices) % 256 == 0 else 128

    def by_head(value):
        return value.reshape(value.shape[0], -1, HD).transpose(1, 0, 2)

    def exchange(value):
        return lax.all_to_all(value, "aa", 0, 0, tiled=True)

    gathered = lax.all_gather(grad_out, "ba", axis=1, tiled=True)
    all_seg = lax.all_gather(segment_ids, "aa", axis=0, tiled=True)
    low, starts = document_starts(all_seg, block)
    send = jnp.concatenate(
        [by_head(query), jnp.repeat(by_head(keys), 2, axis=0), jnp.repeat(by_head(values), 2, axis=0)], axis=2
    )
    qkv = exchange(send).reshape(-1, 3 * HD)
    lse = head_stats(low, starts, qkv, scaling)
    gathered, lse = lax.optimization_barrier((gathered, lse))
    dout = exchange(by_head(project_back(gathered, w_out).astype(jnp.bfloat16))).reshape(-1, HD)
    grad_q, grad_kv = head_grads(low, starts, lse, qkv, dout, scaling)
    half = tok_count // 2
    odd = lax.axis_index("aa") % 2
    grad_kv = grad_kv.reshape(heads, 2, half, 2 * HD)
    own = lax.dynamic_index_in_dim(grad_kv, odd, 1, keepdims=False)
    other = lax.dynamic_index_in_dim(grad_kv, 1 - odd, 1, keepdims=False)
    other = lax.ppermute(other, "aa", [(source, source ^ 1) for source in range(seq_devices)])
    back_q = exchange(grad_q.reshape(heads, tok_count, HD))
    own = (own.astype(jnp.float32) + other.astype(jnp.float32)).astype(jnp.bfloat16)
    back_q, own = lax.optimization_barrier((back_q, own))
    back_kv = exchange(own).reshape(groups, 2 * half, 2 * HD).transpose(1, 0, 2)
    grad_q = back_q.transpose(1, 0, 2).reshape(tok_count, heads * HD)
    grad_k = back_kv[:, :, 0:HD].reshape(tok_count, groups * HD)
    grad_v = back_kv[:, :, HD:].reshape(tok_count, groups * HD)
    part = project_back(grad_q, w_query) + project_back(grad_k, w_key) + project_back(grad_v, w_value)
    return lax.psum_scatter(part.astype(jnp.bfloat16), "ba", scatter_dimension=1, tiled=True)


def solution(mesh):
    return jax.shard_map(
        local,
        mesh=mesh,
        in_specs=(
            P("aa", "ba"),
            P("aa", "ba"),
            P("aa", "ba"),
            P("aa", "ba"),
            P("aa"),
            P(None, "ba"),
            P(None, "ba"),
            P(None, "ba"),
            P("ba", None),
        ),
        out_specs=P("aa", "ba"),
        check_vma=False,
    )
```

profile of v0, /device:TPU:8, one launch (start us, length us, event | category | flops | bytes accessed | tf_op | source)
XLA Modules:
  0.0 275.4 jit_solution(5292813268666439086)
XLA Ops:
  6.5 0.0 copy-start
  6.5 0.7 all-gather.3.cloned.1.call-update
  7.3 1.1 reshape.51
  8.4 0.1 copy.36
  8.4 1.1 reshape.53
  9.5 0.1 copy.37
  9.6 0.1 bitcast_bitcast_fusion.1
  9.7 0.1 broadcast_in_dim.25
  9.8 0.0 copy-start.4
  9.9 0.1 broadcast_in_dim.26
  10.0 1.8 pad_maximum_fusion
  11.7 3.7 %all-to-all-start = ((bf16[8,384,384]{2,1,0:T(8,128)(2,1)}), bf16[8,384,384]{2,1,0:T(8,128)(2,1)S(1)}, u32[]{:S(2)}, u32[]{:S(2)}) async-start(bf16[8,384,384]{2,1,0:T(8,128)(2,1)} %pad_maximum_fusion), calls=%async_computation | async-start | bytes 4718592 | tf_op jit(solution)/shard_map/all_to_all | solution.py:315
  15.5 32.5 %all-gather = s32[8,1,384]{2,1,0:T(1,128)S(1)} all-gather(s32[1,1,384]{2,1,0:T(1,128)S(1)} %reshape.65), channel_id=1, replica_groups=mesh['aa'=8,'ba'=4] {'aa'}, dimensions={0}, use_global_device_ids=true | all-gather | bytes 13824 | tf_op jit(solution)/shard_map/all_gather | solution.py:318
  47.9 0.1 convert_reduce_fusion
  48.1 0.1 select_reduce_fusion
  48.2 0.1 slice_reduce_fusion
  48.3 0.0 all-to-all-done
  48.3 14.1 %stats.1.lse_ref = f32[12,256]{1,0:T(8,128)S(1)} custom-call(s32[12]{0:T(128)S(1)} %and_select_fusion.low_ref, s32[12,256]{1,0:T(8,128)S(1)} %reshape.49.start_ref, bf16[3072,384]{1,0:T(8,128)(2,1)S(1)} %bitcast.47), custom_call_target="tpu_custom_call" | custom-call | flops 1207959552 | bytes 2359296 | tf_op jit(solution)/shard_map/stats/pallas_call | solution.py:267
  62.5 24.6 %all-gather.3.cloned.1.call-done = bf16[384,5376]{0,1:T(8,128)(2,1)} async-done(((bf16[384,1344]{0,1:T(8,128)(2,1)}), bf16[384,5376]{0,1:T(8,128)(2,1)}) %all-gather.3.cloned.1.call-update) | async-done | bytes 4128784 | tf_op jit(solution)/shard_map/all_gather | solution.py:317
  87.1 9.9 %fusion.2 = bf16[48,8,8,128]{3,2,1,0:T(8,128)(2,1)S(1)} fusion(bf16[384,5376]{0,1:T(8,128)(2,1)} %all-gather.3.cloned.1.call-done, bf16[1024,5376]{1,0:T(8,128)(2,1)} %param.17), kind=kOutput, calls=%fused_computation.7 | convolution fusion | flops 4228251648 | bytes 15925248 | tf_op jit(solution)/shard_map/dot_general | solution.py:86
  97.0 1.0 copy.48
  98.0 3.9 %all-to-all-start.1 = ((bf16[8,384,128]{2,1,0:T(8,128)(2,1)}), bf16[8,384,128]{2,1,0:T(8,128)(2,1)S(1)}, u32[]{:S(2)}, u32[]{:S(2)}) async-start(bf16[8,384,128]{2,1,0:T(8,128)(2,1)} %bitcast.57), calls=%async_computation.1 | async-start | bytes 1572864 | tf_op jit(solution)/shard_map/all_to_all | solution.py:315
  101.9 12.6 %all-to-all-done.1 = bf16[8,384,128]{2,1,0:T(8,128)(2,1)S(1)} async-done(((bf16[8,384,128]{2,1,0:T(8,128)(2,1)}), bf16[8,384,128]{2,1,0:T(8,128)(2,1)S(1)}, u32[]{:S(2)}, u32[]{:S(2)}) %all-to-all-start.1) | async-done | bytes 786464 | tf_op jit(solution)/shard_map/all_to_all | solution.py:315
  114.4 29.1 %grads.1 = (bf16[3072,128]{1,0:T(8,128)(2,1)S(1)}, bf16[3072,256]{1,0:T(8,128)(2,1)S(1)}) custom-call(s32[12]{0:T(128)S(1)} %and_select_fusion.low_ref, s32[12,256]{1,0:T(8,128)S(1)} %reshape.49.start_ref, f32[12,256]{1,0:T(8,128)S(1)} %stats.1.lse_ref, bf16[3072,384]{1,0:T(8,128)(2,1)S(1)} %bitcast.48, bf16[3072,128]{1,0:T(8,128)(2,1)S(1)} %bitcast.51), custom_call_target="tpu_custom_call" | custom-call | flops 6039797760 | bytes 7077888 | tf_op jit(solution)/shard_map/grads/pallas_call | solution.py:281
  143.6 0.0 copy-start.3
  143.6 1.1 copy-done.2
  144.7 0.1 dynamic-slice_bitcast_fusion
  144.8 0.2 copy-done.3
  145.0 0.0 collective-permute-start
  145.0 2.3 copy.39
  147.2 3.5 %all-to-all-start.2 = ((bf16[8,384,128]{1,2,0:T(8,128)(2,1)}), bf16[8,384,128]{1,2,0:T(8,128)(2,1)S(1)}, u32[]{:S(2)}, u32[]{:S(2)}) async-start(bf16[8,384,128]{1,2,0:T(8,128)(2,1)} %copy.39), calls=%async_computation.2 | async-start | bytes 1572864 | tf_op jit(solution)/shard_map/all_to_all | solution.py:315
  150.8 0.0 collective-permute-done
  150.8 2.2 fusion.1
  153.0 10.3 %all-to-all-done.2 = bf16[8,384,128]{1,2,0:T(8,128)(2,1)S(1)} async-done(((bf16[8,384,128]{1,2,0:T(8,128)(2,1)}), bf16[8,384,128]{1,2,0:T(8,128)(2,1)S(1)}, u32[]{:S(2)}, u32[]{:S(2)}) %all-to-all-start.2) | async-done | bytes 786464 | tf_op jit(solution)/shard_map/all_to_all | solution.py:315
  163.3 3.5 %all-to-all-start.3 = ((bf16[8,192,256]{2,1,0:T(8,128)(2,1)}), bf16[8,192,256]{2,1,0:T(8,128)(2,1)S(1)}, u32[]{:S(2)}, u32[]{:S(2)}) async-start(bf16[8,192,256]{2,1,0:T(8,128)(2,1)} %fusion.1), calls=%async_computation.3 | async-start | bytes 1572864 | tf_op jit(solution)/shard_map/all_to_all | solution.py:315
  166.9 0.2 reduce-scatter.2.cloned.1.call-start
  167.1 10.6 %fusion.4 = f32[384,5376]{0,1:T(8,128)} fusion(bf16[5376,1024]{1,0:T(8,128)(2,1)} %param.14, bf16[384,1024]{0,1:T(8,128)(2,1)S(1)} %bitcast.63), kind=kOutput, calls=%fused_computation.21 | convolution fusion | flops 4227858432 | bytes 20054016 | tf_op jit(solution)/shard_map/dot_general | solution.py:86
  177.7 1.7 all-to-all-done.3
  179.4 0.1 fusion.3
  179.5 0.0 slice-start
  179.5 0.2 copy.42
  179.8 0.2 copy.41
  180.0 0.0 slice-start.1
  180.0 8.4 %convolution_add_fusion.1 = f32[384,5376]{0,1:T(8,128)S(1)} fusion(f32[384,5376]{0,1:T(8,128)} %fusion.4, bf16[5376,512]{1,0:T(8,128)(2,1)} %param.15, bf16[384,512]{0,1:T(8,128)(2,1)S(1)} %bitcast.59), kind=kOutput, calls=%fused_computation.1 | convolution fusion | flops 2115993600 | bytes 22413312 | tf_op jit(solution)/shard_map/dot_general | solution.py:86
  188.4 0.0 copy-start.1
  188.5 4.7 %fusion = bf16[384,5376]{0,1:T(8,128)(2,1)} fusion(f32[384,5376]{0,1:T(8,128)S(1)} %convolution_add_fusion.1, bf16[5376,512]{1,0:T(8,128)(2,1)S(1)} %bitcast.54, bf16[384,512]{0,1:T(8,128)(2,1)S(1)} %bitcast.62), kind=kOutput, calls=%fused_computation.2 | convolution fusion | flops 2118057984 | bytes 18284544 | tf_op jit(solution)/shard_map/dot_general | solution.py:86
  193.1 0.0 reduce-scatter.2.cloned.1.call-update
  193.1 75.4 %reduce-scatter.2.cloned.1.call-done = bf16[384,1344]{0,1:T(8,128)(2,1)} async-done(((bf16[384,5376]{0,1:T(8,128)(2,1)}), bf16[384,1344]{0,1:T(8,128)(2,1)}) %reduce-scatter.2.cloned.1.call-update) | async-done | bytes 1032208 | tf_op jit(solution)/shard_map/reduce_scatter | solution.py:342
  (11 shorter events, 0.0 us)
Async XLA Ops:
  6.5 3.0 %copy-start = (bf16[384,1024]{1,0:T(8,128)(2,1)S(1)}, bf16[384,1024]{1,0:T(8,128)(2,1)}, u32[]{:S(2)}) copy-start(bf16[384,1024]{1,0:T(8,128)(2,1)} %param.9) | copy-start | bytes 2359300
  6.5 80.6 %all-gather.3.cloned.1.call-start = ((), (), s32[]{:S(2)}) async-start(), calls=%async_computation.5 | async-start | bytes 5160960 | tf_op jit(solution)/shard_map/all_gather | solution.py:317
  9.8 5.6 %copy-start.4 = (s32[384]{0:T(512)S(1)}, s32[384]{0:T(512)}, u32[]{:S(2)}) copy-start(s32[384]{0:T(512)} %param.13) | copy-start | bytes 4612
  11.7 36.6 %all-to-all-start = ((bf16[8,384,384]{2,1,0:T(8,128)(2,1)}), bf16[8,384,384]{2,1,0:T(8,128)(2,1)S(1)}, u32[]{:S(2)}, u32[]{:S(2)}) async-start(bf16[8,384,384]{2,1,0:T(8,128)(2,1)} %pad_maximum_fusion), calls=%async_computation | async-start | bytes 4718592 | tf_op jit(solution)/shard_map/all_to_all | solution.py:315
  98.0 16.4 %all-to-all-start.1 = ((bf16[8,384,128]{2,1,0:T(8,128)(2,1)}), bf16[8,384,128]{2,1,0:T(8,128)(2,1)S(1)}, u32[]{:S(2)}, u32[]{:S(2)}) async-start(bf16[8,384,128]{2,1,0:T(8,128)(2,1)} %bitcast.57), calls=%async_computation.1 | async-start | bytes 1572864 | tf_op jit(solution)/shard_map/all_to_all | solution.py:315
  143.6 1.2 copy-start.2
  143.6 1.4 copy-start.3
  145.0 5.9 %collective-permute-start = (bf16[8,192,256]{2,1,0:T(8,128)(2,1)S(1)}, bf16[8,192,256]{2,1,0:T(8,128)(2,1)S(1)}, u32[]{:S(2)}, u32[]{:S(2)}) collective-permute-start(bf16[8,192,256]{2,1,0:T(8,128)(2,1)S(1)} %dynamic-slice_bitcast_fusion), channel_id=1, source_target_pairs={{0,4},{4,0},{8,12},{12,8},{16,20},{20,16},{24,28},{28,24},{1,5},{5... | collective-permute-start | bytes 2359304 | tf_op jit(solution)/shard_map/ppermute | solution.py:333
  147.2 16.1 %all-to-all-start.2 = ((bf16[8,384,128]{1,2,0:T(8,128)(2,1)}), bf16[8,384,128]{1,2,0:T(8,128)(2,1)S(1)}, u32[]{:S(2)}, u32[]{:S(2)}) async-start(bf16[8,384,128]{1,2,0:T(8,128)(2,1)} %copy.39), calls=%async_computation.2 | async-start | bytes 1572864 | tf_op jit(solution)/shard_map/all_to_all | solution.py:315
  163.3 16.1 %all-to-all-start.3 = ((bf16[8,192,256]{2,1,0:T(8,128)(2,1)}), bf16[8,192,256]{2,1,0:T(8,128)(2,1)S(1)}, u32[]{:S(2)}, u32[]{:S(2)}) async-start(bf16[8,192,256]{2,1,0:T(8,128)(2,1)} %fusion.1), calls=%async_computation.3 | async-start | bytes 1572864 | tf_op jit(solution)/shard_map/all_to_all | solution.py:315
  166.9 101.7 %reduce-scatter.2.cloned.1.call-start = ((), (), s32[]{:S(2)}) async-start(), calls=%async_computation.6 | async-start | bytes 5160960 | tf_op jit(solution)/shard_map/reduce_scatter | solution.py:342
  179.5 8.9 %slice-start = ((s8[5505024]{0:T(1024)(128)(4,1)}), s8[1310720]{0:T(1024)(128)(4,1)S(1)}, s32[]{:S(2)}) async-start(s8[5505024]{0:T(1024)(128)(4,1)} %bitcast.53), calls=%async_computation.7 | async-start | bytes 2621440
  180.0 8.4 %slice-start.1 = ((s8[5505024]{0:T(1024)(128)(4,1)}), s8[4194304]{0:T(1024)(128)(4,1)S(1)}, s32[]{:S(2)}) async-start(s8[5505024]{0:T(1024)(128)(4,1)} %bitcast.53), calls=%async_computation.8 | async-start | bytes 8388608
  188.4 80.1 %copy-start.1 = (bf16[384,1024]{1,0:T(8,128)(2,1)S(1)}, bf16[384,1024]{1,0:T(8,128)(2,1)}, u32[]{:S(2)}) copy-start(bf16[384,1024]{1,0:T(8,128)(2,1)} %param.9) | copy-start | bytes 2359300
Sparse Core Ops, SparseCore 0:
  8.9 78.1 all-gather.2
  193.3 75.2 reduce-scatter.1
where the time goes:
time: 273 us; the launch traced here: 275 us
  waiting for transfers between devices  125 us (46%)
  Pallas kernels  43.2 us (16%)
  matrix products  33.5 us (12%)
  blocking collectives  32.5 us (12%)
  starting transfers between devices  14.9 us (5%)
  between operations  13.6 us (5%)
  local copies, waits for them, and re-layouts  8.06 us (3%)
  other arithmetic  4.24 us (2%)
    reduce_scatter x1, waiting for transfers between devices, local(): lax.psum_scatter(part.astype(jnp.bfloat16), 'ba', scatter_dimension=1, ti...  75.4 us
    dot_general x4, matrix products, project_back(): lax.dot_general(grad, weight, (((1,), (1,)), ((), ())), preferred_element...  33.5 us
    all_gather x1, blocking collectives, local(): all_seg = lax.all_gather(segment_ids, 'aa', axis=0, tiled=True)  32.5 us
    pallas_call x1, Pallas kernels, head_grads(): pl.pallas_call(functools.partial(grads_kernel, block, scaling), out_shape...  29.1 us
    all_gather x1, waiting for transfers between devices, local(): gathered = lax.all_gather(grad_out, 'ba', axis=1, tiled=True)  24.6 us
    all_to_all x4, waiting for transfers between devices, exchange(): return lax.all_to_all(value, 'aa', 0, 0, tiled=True)  24.5 us
    all_to_all x4, starting transfers between devices, exchange(): return lax.all_to_all(value, 'aa', 0, 0, tiled=True)  14.7 us
    pallas_call x1, Pallas kernels, head_stats(): pl.pallas_call(functools.partial(stats_kernel, block, scaling), out_shape...  14.1 us
  transfers between devices with their start and end apart: 7, of which 5 were waited for; matrix products, arithmetic and copies ran while one was open for 7% of the time, Pallas kernels for 5%

commit v1 on v0

v1 whole, which is shorter than its diff:
```python
import functools

import jax
import jax.numpy as jnp
from jax import lax
from jax.experimental import pallas as pl
from jax.experimental.pallas import tpu as pltpu
from jax.sharding import PartitionSpec as P

D = 5376
HQ = 32
HD = 128
DOCS = 6


NEG_FILL = -1e30


def from_behind(value, axis, steps):
    count = lax.axis_size(axis)
    pairs = [(source, (source + steps) % count) for source in range(count)]
    return lax.ppermute(value, axis, pairs)


def block_scores(query, dout, keys, values, query_pos, query_seg, key_pos, key_seg, scaling):
    row_count = query.shape[0]
    col_count = keys.shape[0]
    groups = keys.shape[1] // HD
    query_four = query.reshape(row_count, groups, 2, HD)
    dout_four = dout.reshape(row_count, groups, 2, HD)
    key_three = keys.reshape(col_count, groups, HD)
    value_three = values.reshape(col_count, groups, HD)
    scores = (
        jnp.einsum("iagd,jad->agij", query_four, key_three, preferred_element_type=jnp.float32)
        * scaling
    )
    dprobs = jnp.einsum(
        "iagd,jad->agij", dout_four, value_three, preferred_element_type=jnp.float32
    )
    allowed = (key_pos[None, :] <= query_pos[:, None]) & (key_seg[None, :] == query_seg[:, None])
    return (scores, dprobs, allowed, query_four, dout_four, key_three)


def forward_stats(
    query, dout, keys, values, query_pos, query_seg, key_pos, key_seg, scaling, state
):
    run_max, run_sum, run_dot = state
    scores, dprobs, allowed, unused_q, unused_d, unused_k = block_scores(
        query, dout, keys, values, query_pos, query_seg, key_pos, key_seg, scaling
    )
    masked = jnp.where(allowed, scores, NEG_FILL)
    new_max = jnp.maximum(run_max, jnp.max(masked, axis=-1))
    expo = jnp.where(allowed, jnp.exp(scores - new_max[..., None]), 0.0)
    return (new_max, jnp.sum(expo, axis=-1), jnp.sum(expo * dprobs, axis=-1))


def block_grads(
    query, dout, row_lse, row_delta, keys, values, query_pos, query_seg, key_pos, key_seg, scaling
):
    scores, dprobs, allowed, query_four, dout_four, key_three = block_scores(
        query, dout, keys, values, query_pos, query_seg, key_pos, key_seg, scaling
    )
    softmax_w = jnp.where(allowed, jnp.exp(scores - row_lse[..., None]), 0.0)
    dscores = softmax_w * (dprobs - row_delta[..., None])
    softmax_low = softmax_w.astype(jnp.bfloat16)
    dscores_low = dscores.astype(jnp.bfloat16)
    grad_v = jnp.einsum(
        "agij,iagd->jad", softmax_low, dout_four, preferred_element_type=jnp.float32
    )
    grad_k = (
        jnp.einsum("agij,iagd->jad", dscores_low, query_four, preferred_element_type=jnp.float32)
        * scaling
    )
    grad_q = (
        jnp.einsum("agij,jad->iagd", dscores_low, key_three, preferred_element_type=jnp.float32)
        * scaling
    )
    return (
        grad_q.reshape(query.shape[0], -1),
        grad_k.reshape(keys.shape[0], -1),
        grad_v.reshape(keys.shape[0], -1),
    )


def project_back(grad, weight):
    return lax.dot_general(
        grad, weight, (((1,), (1,)), ((), ())), preferred_element_type=jnp.float32
    )


def local_ring(query, keys, values, grad_out, segment_ids, w_query, w_key, w_value, w_out):
    seq_devices = lax.axis_size("aa")
    own_index = lax.axis_index("aa")
    tok_count = query.shape[0]
    scaling = (D / HQ) ** (-0.5)
    groups = keys.shape[1] // HD
    all_seg = lax.all_gather(segment_ids, "aa", axis=0, tiled=True)
    dout = project_back(lax.all_gather(grad_out, "ba", axis=1, tiled=True), w_out).astype(
        jnp.bfloat16
    )
    offsets = lax.iota(jnp.int32, tok_count)
    own_pos = own_index * tok_count + offsets
    own_seg = lax.dynamic_slice_in_dim(all_seg, own_index * tok_count, tok_count)
    stat_shape = (groups, 2, tok_count)
    stats_start = (
        jnp.full(stat_shape, NEG_FILL, jnp.float32),
        jnp.zeros(stat_shape, jnp.float32),
        jnp.zeros(stat_shape, jnp.float32),
    )
    piece = (
        lax.all_gather(keys, "aa", axis=0, tiled=True),
        lax.all_gather(values, "aa", axis=0, tiled=True),
    )
    width = piece[0].shape[0]
    key_pos = lax.iota(jnp.int32, width)
    key_seg = all_seg
    run_max, run_sum, run_dot = forward_stats(
        query, dout, piece[0], piece[1], own_pos, own_seg, key_pos, key_seg, scaling, stats_start
    )
    row_lse = run_max + jnp.log(run_sum)
    row_delta = run_dot / run_sum
    zero_q = jnp.zeros(query.shape, jnp.float32)
    zero_k = jnp.zeros(keys.shape, jnp.float32)

    def step_keys(step_index, state):
        (keys_now, values_now), (dk_now, dv_now), grad_q = state
        anchor = (own_index - step_index) % seq_devices
        key_pos = anchor * tok_count + offsets
        key_seg = lax.dynamic_slice_in_dim(all_seg, anchor * tok_count, tok_count)
        add_q, add_k, add_v = block_grads(
            query,
            dout,
            row_lse,
            row_delta,
            keys_now,
            values_now,
            own_pos,
            own_seg,
            key_pos,
            key_seg,
            scaling,
        )
        bundle_next = from_behind((keys_now, values_now), "aa", 1)
        sums_next = (
            from_behind((dk_now + add_k).astype(jnp.bfloat16), "aa", 1).astype(jnp.float32),
            from_behind((dv_now + add_v).astype(jnp.bfloat16), "aa", 1).astype(jnp.float32),
        )
        return (bundle_next, sums_next, grad_q + add_q)

    initial = ((keys, values), (zero_k, zero_k), zero_q)
    final = lax.fori_loop(0, seq_devices, step_keys, initial)
    grad_q = final[2]
    grad_k = final[1][0]
    grad_v = final[1][1]
    partial_value = (
        project_back(grad_q.astype(jnp.bfloat16), w_query)
        + project_back(grad_k.astype(jnp.bfloat16), w_key)
        + project_back(grad_v.astype(jnp.bfloat16), w_value)
    )
    return lax.psum_scatter(
        partial_value.astype(jnp.bfloat16), "ba", scatter_dimension=1, tiled=True
    )


def fold_rows(value, op):
    return op(value.reshape(-1, 8, value.shape[1]), axis=0)


CONTRACT_LAST = (((1,), (1,)), ((), ()))


WHOLE = pl.BlockSpec(memory_space=pltpu.VMEM)


MESH = pl.DeviceIdType.MESH
HBM = pl.BlockSpec(memory_space=pl.ANY)
SUBS = 3


def scatter_kernel(planes, gq_ref, gkv_ref, wq_ref, wk_ref, wv_ref, out_ref, wqb, wkb, wvb, sbuf, rbuf, total_ref, wsem, ssem, rsem):
    z = lax.axis_index("ba")
    barrier = pltpu.get_barrier_semaphore()
    last = planes - 1
    low = z > 0
    high = z < last

    @pl.when(low)
    def _():
        pl.semaphore_signal(barrier, inc=1, device_id={"ba": z - 1}, device_id_type=MESH)

    @pl.when(high)
    def _():
        pl.semaphore_signal(barrier, inc=1, device_id={"ba": z + 1}, device_id_type=MESH)

    rows = out_ref.shape[0]
    sub_rows = rows // SUBS

    def target(side, step):
        return step if side == 0 else last - step

    def sends(side, step):
        return step < z if side == 0 else step < last - z

    def weight_copies(feature, slot):
        span = pl.ds(pl.multiple_of(feature * rows, 16), rows)
        return [
            pltpu.make_async_copy(src.at[span], dst.at[slot], wsem.at[slot, part])
            for part, (src, dst) in enumerate(((wq_ref, wqb), (wk_ref, wkb), (wv_ref, wvb)))
        ]

    order = [(step, side) for step in range(last) for side in range(2)]

    def slot_of(side, step):
        return step if side == 0 else last - step

    for step, side in order:
        @pl.when(sends(side, step))
        def _(step=step, side=side):
            for copy in weight_copies(target(side, step), slot_of(side, step)):
                copy.start()
    for copy in weight_copies(z, z):
        copy.start()

    pl.semaphore_wait(barrier, jnp.minimum(z, 1) + jnp.minimum(last - z, 1))

    half = gkv_ref.shape[1] // 2

    def part(slot, sub):
        span = pl.ds(sub * sub_rows, sub_rows)
        acc = jnp.dot(wqb[slot, span, :], gq_ref[...], preferred_element_type=jnp.float32)
        acc += lax.dot_general(wkb[slot, span, :], gkv_ref[:, 0:half], CONTRACT_LAST, preferred_element_type=jnp.float32)
        return acc + lax.dot_general(wvb[slot, span, :], gkv_ref[:, half:], CONTRACT_LAST, preferred_element_type=jnp.float32)

    def hop(side, step, sub):
        span = pl.ds(sub * sub_rows, sub_rows)
        return pltpu.make_async_remote_copy(
            src_ref=sbuf.at[side, step, span],
            dst_ref=rbuf.at[side, step, span],
            send_sem=ssem.at[side, step, sub],
            recv_sem=rsem.at[side, step, sub],
            device_id={"ba": z - 1 if side == 0 else z + 1},
            device_id_type=MESH,
        )

    for step, side in order:
        behind = high if side == 0 else low

        @pl.when(sends(side, step))
        def _(step=step, side=side, behind=behind):
            slot = slot_of(side, step)
            for copy in weight_copies(target(side, step), slot):
                copy.wait()
            for sub in range(SUBS):
                span = pl.ds(sub * sub_rows, sub_rows)
                acc = part(slot, sub)

                @pl.when(behind)
                def _():
                    hop(side, step, sub).wait_recv()
                    sbuf[side, step, span, :] = (acc + rbuf[side, step, span, :].astype(jnp.float32)).astype(jnp.bfloat16)

                @pl.when(jnp.logical_not(behind))
                def _():
                    sbuf[side, step, span, :] = acc.astype(jnp.bfloat16)

                hop(side, step, sub).start()

    for copy in weight_copies(z, z):
        copy.wait()
    for sub in range(SUBS):
        span = pl.ds(sub * sub_rows, sub_rows)
        total_ref[span, :] = part(z, sub)
    for sub in range(SUBS):
        span = pl.ds(sub * sub_rows, sub_rows)
        for side in range(2):
            for step in range(last):
                here = (z == target(side, step)) & (high if side == 0 else low)

                @pl.when(here)
                def _(side=side, step=step):
                    hop(side, step, sub).wait_recv()
                    total_ref[span, :] += rbuf[side, step, span, :].astype(jnp.float32)

        out_ref[span, :] = total_ref[span, :].astype(jnp.bfloat16)

    for step, side in order:
        @pl.when(sends(side, step))
        def _(step=step, side=side):
            for sub in range(SUBS):
                hop(side, step, sub).wait_send()


def project_scatter(gq, gkv, w_query, w_key, w_value):
    planes = lax.axis_size("ba")
    rows = w_query.shape[0] // planes
    tokens = gq.shape[1]
    last = planes - 1
    return pl.pallas_call(
        functools.partial(scatter_kernel, planes),
        out_shape=jax.ShapeDtypeStruct((rows, tokens), jnp.bfloat16),
        in_specs=[WHOLE, WHOLE, HBM, HBM, HBM],
        out_specs=WHOLE,
        scratch_shapes=[
            pltpu.VMEM((planes, rows, w_query.shape[1]), jnp.bfloat16),
            pltpu.VMEM((planes, rows, w_key.shape[1]), jnp.bfloat16),
            pltpu.VMEM((planes, rows, w_value.shape[1]), jnp.bfloat16),
            pltpu.VMEM((2, last, rows, tokens), jnp.bfloat16),
            pltpu.VMEM((2, last, rows, tokens), jnp.bfloat16),
            pltpu.VMEM((rows, tokens), jnp.float32),
            pltpu.SemaphoreType.DMA((planes, 3)),
            pltpu.SemaphoreType.DMA((2, last, SUBS)),
            pltpu.SemaphoreType.DMA((2, last, SUBS)),
        ],
        compiler_params=pltpu.CompilerParams(
            collective_id=1, has_side_effects=True, vmem_limit_bytes=56 * 1024 * 1024
        ),
        name="project_scatter",
    )(gq, gkv, w_query, w_key, w_value)


CHUNK = 128
LOG2E = 1.4426950408889634


def attention_kernel(peers, planes, chunks, scaling, q_ref, k_ref, v_ref, seg_ref, g_ref, w_ref, gq_ref, gkv_ref,
                     wbuf, fbuf, qa, ka, va, kt, vt, segs, starts_ref, s_ref, p_ref, ot_ref, inv_ref, dvk_ref,
                     dsend, drecv, gqs, pair_out, pair_in, kvs,
                     local_sem, own_sem, ag_s, ag_r, x_s, x_r, d_s, d_r, gq_s, gq_r, pr_s, pr_r, kv_s, kv_r):
    me = lax.axis_index("aa")
    z = lax.axis_index("ba")
    last = planes - 1
    tok = q_ref.shape[0]
    feats = g_ref.shape[0]
    half = gkv_ref.shape[1] // 2
    barrier = pltpu.get_barrier_semaphore()

    def lanes(index):
        return pl.ds(pl.multiple_of(index * HD, HD), HD)

    def rows_of(index):
        return pl.ds(pl.multiple_of(index * tok, tok), tok)

    def peer(r):
        return lax.rem(me + r, peers)

    for r in range(1, peers):
        pl.semaphore_signal(barrier, inc=1, device_id={"aa": peer(r)}, device_id_type=MESH)
    for r in range(1, planes):
        pl.semaphore_signal(barrier, inc=1, device_id={"ba": lax.rem(z + r, planes)}, device_id_type=MESH)

    def own_copies():
        return [
            pltpu.make_async_copy(g_ref, fbuf.at[pl.ds(pl.multiple_of(z * feats, 16), feats)], own_sem.at[0]),
            pltpu.make_async_copy(q_ref.at[:, lanes(me)], qa.at[rows_of(me)], own_sem.at[1]),
            pltpu.make_async_copy(k_ref.at[:, lanes(me // 2)], ka.at[rows_of(me)], own_sem.at[2]),
            pltpu.make_async_copy(v_ref.at[:, lanes(me // 2)], va.at[rows_of(me)], own_sem.at[3]),
            pltpu.make_async_copy(seg_ref, segs.at[me], own_sem.at[4]),
        ]

    weight_copy = pltpu.make_async_copy(w_ref, wbuf, local_sem)
    for copy in own_copies():
        copy.start()
    pl.semaphore_wait(barrier, peers + planes - 2)

    def gather(side, c, s):
        source = z - s if side == 0 else z + s
        span = pl.ds(pl.multiple_of(source * feats, 16), feats)
        cols = pl.ds(c * CHUNK, CHUNK)
        return pltpu.make_async_remote_copy(
            src_ref=g_ref.at[:, cols] if s == 0 else fbuf.at[span, cols],
            dst_ref=fbuf.at[span, cols],
            send_sem=ag_s.at[side, c, s],
            recv_sem=ag_r.at[side, c, s],
            device_id={"ba": z + 1 if side == 0 else z - 1},
            device_id_type=MESH,
        )

    def arrival(side, c, s):
        source = z - 1 - s if side == 0 else z + 1 + s
        span = pl.ds(pl.multiple_of(source * feats, 16), feats)
        cols = pl.ds(c * CHUNK, CHUNK)
        return pltpu.make_async_remote_copy(
            src_ref=fbuf.at[span, cols],
            dst_ref=fbuf.at[span, cols],
            send_sem=ag_s.at[side, c, s],
            recv_sem=ag_r.at[side, c, s],
            device_id={"ba": z + 1 if side == 0 else z - 1},
            device_id_type=MESH,
        )

    def gather_sends(side, s):
        return (z >= s) & (z < last) if side == 0 else (z + s <= last) & (z > 0)

    def relay(c, s):
        for side in range(2):
            @pl.when(gather_sends(side, s))
            def _(side=side):
                if s > 0:
                    arrival(side, c, s - 1).wait_recv()
                gather(side, c, s).start()

    def finish_gather(c):
        for side in range(2):
            for s in range(last):
                @pl.when((z == last) if side == 0 else (z == 0))
                def _(side=side, s=s):
                    arrival(side, c, s).wait_recv()

    def exchange(kind, to, sender, peer_sem):
        shard = (q_ref.at[:, lanes(to)], k_ref.at[:, lanes(to // 2)], v_ref.at[:, lanes(to // 2)], seg_ref)[kind]
        land = (qa.at[rows_of(sender)], ka.at[rows_of(sender)], va.at[rows_of(sender)], segs.at[sender])[kind]
        return pltpu.make_async_remote_copy(
            src_ref=shard,
            dst_ref=land,
            send_sem=x_s.at[kind, peer_sem],
            recv_sem=x_r.at[kind, sender],
            device_id={"aa": to},
            device_id_type=MESH,
        )

    relay(0, 0)
    relay(1, 0)
    for r in range(1, peers):
        exchange(3, peer(r), me, r).start()
    for r in range(1, peers):
        for kind in range(3):
            exchange(kind, peer(r), me, r).start()
    weight_copy.start()
    dvk_ref[...] = jnp.zeros_like(dvk_ref)
    relay(0, 1)
    relay(1, 1)
    for copy in own_copies():
        copy.wait()
    for r in range(1, peers):
        exchange(3, me, peer(r), r).wait_recv()

    ids = segs[...]
    starts = jnp.zeros(ids.shape, jnp.float32)
    for doc in range(1, DOCS):
        before = jnp.sum(jnp.where(ids < doc, 1.0, 0.0), axis=(0, 2), keepdims=True)
        starts = jnp.where(ids == doc, before, starts)
    starts_ref[...] = starts
    relay(0, 2)
    relay(2, 0)

    def tri(m):
        return m * (m + 1) // 2 * CHUNK

    def stats(c, first):
        def block(a, carry):
            m = chunks * a + c
            if first:
                @pl.when(a != me)
                def _():
                    for kind in range(3):
                        exchange(kind, me, a, 0).wait_recv()

                kt[:, rows_of(a)] = ka[rows_of(a), :].astype(jnp.float32).T.astype(jnp.bfloat16)
                vt[:, rows_of(a)] = va[rows_of(a), :].astype(jnp.float32).T.astype(jnp.bfloat16)
            query = qa[pl.ds(pl.multiple_of(m * CHUNK, CHUNK), CHUNK), :]
            begin = starts_ref[a, :, c * CHUNK : (c + 1) * CHUNK]

            def scores(at, size, diagonal):
                span = pl.ds(pl.multiple_of(at, CHUNK), size)
                s = lax.dot_general(ka[span, :], query, CONTRACT_LAST, preferred_element_type=jnp.float32)
                key = lax.broadcasted_iota(jnp.int32, (size, CHUNK), 0)
                if diagonal:
                    allowed = key <= c * CHUNK + lax.broadcasted_iota(jnp.int32, (size, CHUNK), 1)
                    allowed &= (key + at).astype(jnp.float32) >= begin
                else:
                    allowed = (key + at).astype(jnp.float32) >= begin
                s = jnp.where(allowed, s * (scaling * LOG2E), NEG_FILL)
                s_ref[span, :] = s
                return fold_rows(s, jnp.max)

            top = lax.fori_loop(0, a, lambda u, t: jnp.maximum(t, scores(u * tok, tok, False)),
                                jnp.full((8, CHUNK), NEG_FILL, jnp.float32))
            size = (c + 1) * CHUNK
            top = jnp.maximum(top, scores(a * tok, size, True))
            top = jnp.max(top, axis=0, keepdims=True)

            def weights(at, size, state):
                total, out = state
                span = pl.ds(pl.multiple_of(at, CHUNK), size)
                p = jnp.exp2(s_ref[span, :] - top)
                low = p.astype(jnp.bfloat16)
                p_ref[pl.ds(pl.multiple_of(tri(m) + at, CHUNK), size), :] = low
                return (total + fold_rows(p, jnp.sum),
                        out + jnp.dot(vt[:, span], low, preferred_element_type=jnp.float32))

            state = (jnp.zeros((8, CHUNK), jnp.float32), jnp.zeros((HD, CHUNK), jnp.float32))
            state = lax.fori_loop(0, a, lambda u, st: weights(u * tok, tok, st), state)
            total, out = weights(a * tok, size, state)
            inverse = 1.0 / jnp.sum(total, axis=0, keepdims=True)
            inv_ref[m] = inverse
            ot_ref[m] = out * inverse
            return carry

        lax.fori_loop(0, peers, block, 0)

    def dout_send(c, to):
        return pltpu.make_async_remote_copy(
            src_ref=dsend.at[c, to],
            dst_ref=drecv.at[c, me],
            send_sem=d_s.at[c, to],
            recv_sem=d_r.at[c, me],
            device_id={"aa": to},
            device_id_type=MESH,
        )

    def dout_arrival(c, sender):
        return pltpu.make_async_remote_copy(
            src_ref=dsend.at[c, sender],
            dst_ref=drecv.at[c, sender],
            send_sem=d_s.at[c, sender],
            recv_sem=d_r.at[c, sender],
            device_id={"aa": sender},
            device_id_type=MESH,
        )

    def project(c):
        finish_gather(c)
        pair = 2

        def heads(i, carry):
            span = pl.ds(pl.multiple_of(i * (pair * HD), HD), pair * HD)
            out = jnp.dot(wbuf[span, :], fbuf[:, c * CHUNK : (c + 1) * CHUNK], preferred_element_type=jnp.float32)
            for j in range(pair):
                to = i * pair + j
                dsend[c, to] = out[j * HD : (j + 1) * HD, :].astype(jnp.bfloat16)

                @pl.when(to != me)
                def _():
                    dout_send(c, to).start()

            return carry

        lax.fori_loop(0, peers // pair, heads, 0)
        drecv[c, me] = dsend[c, me]

    def gq_copy(c, to):
        return pltpu.make_async_remote_copy(
            src_ref=gqs.at[c, to],
            dst_ref=gq_ref.at[lanes(me), pl.ds(c * CHUNK, CHUNK)],
            send_sem=gq_s.at[c, to],
            recv_sem=gq_r.at[c, me],
            device_id={"aa": to},
            device_id_type=MESH,
        )

    def gq_arrival(c, sender):
        return pltpu.make_async_remote_copy(
            src_ref=gqs.at[c, sender],
            dst_ref=gq_ref.at[lanes(sender), pl.ds(c * CHUNK, CHUNK)],
            send_sem=gq_s.at[c, sender],
            recv_sem=gq_r.at[c, sender],
            device_id={"aa": sender},
            device_id_type=MESH,
        )

    def gq_local(c):
        return pltpu.make_async_copy(gqs.at[c, me], gq_ref.at[lanes(me), pl.ds(c * CHUNK, CHUNK)], own_sem.at[c])

    def grads(c):
        def block(a, carry):
            m = chunks * a + c

            @pl.when(a != me)
            def _():
                dout_arrival(c, a).wait_recv()

            query = qa[pl.ds(pl.multiple_of(m * CHUNK, CHUNK), CHUNK), :]
            dout = (drecv[c, a].astype(jnp.float32) * inv_ref[m]).astype(jnp.bfloat16)
            delta = jnp.sum(dout.astype(jnp.float32) * ot_ref[m], axis=0, keepdims=True)

            def unit(at, size, grad_q):
                span = pl.ds(pl.multiple_of(at, CHUNK), size)
                p = p_ref[pl.ds(pl.multiple_of(tri(m) + at, CHUNK), size), :]
                dp = jnp.dot(va[span, :], dout, preferred_element_type=jnp.float32)
                ds = (p.astype(jnp.float32) * (dp - delta)).astype(jnp.bfloat16)
                dvk_ref[span, 0:HD] += lax.dot_general(p, dout, CONTRACT_LAST, preferred_element_type=jnp.float32)
                dvk_ref[span, HD:] += jnp.dot(ds, query, preferred_element_type=jnp.float32)
                return grad_q + jnp.dot(kt[:, span], ds, preferred_element_type=jnp.float32)

            grad_q = lax.fori_loop(0, a, lambda u, t: unit(u * tok, tok, t), jnp.zeros((HD, CHUNK), jnp.float32))
            grad_q = unit(a * tok, (c + 1) * CHUNK, grad_q)
            gqs[c, a] = (grad_q * scaling).astype(jnp.bfloat16)

            @pl.when(a != me)
            def _():
                gq_copy(c, a).start()

            return carry

        lax.fori_loop(0, peers, block, 0)
        gq_local(c).start()

    stats(0, True)
    relay(1, 2)
    stats(1, False)
    relay(2, 1)
    weight_copy.wait()
    project(0)
    stats(2, False)
    relay(2, 2)
    project(1)
    grads(0)
    grads(1)
    project(2)
    grads(2)

    odd = lax.rem(me, 2)
    partner = me + 1 - 2 * odd
    pair_copy = pltpu.make_async_remote_copy(
        src_ref=pair_out, dst_ref=pair_in, send_sem=pr_s, recv_sem=pr_r, device_id={"aa": partner}, device_id_type=MESH
    )

    @pl.when(odd == 0)
    def _():
        pair_out[...] = dvk_ref[:, 0:HD].astype(jnp.bfloat16)

    @pl.when(odd == 1)
    def _():
        pair_out[...] = (dvk_ref[:, HD:] * scaling).astype(jnp.bfloat16)

    pair_copy.start()
    pair_copy.wait_recv()

    @pl.when(odd == 0)
    def _():
        kvs[...] = (dvk_ref[:, HD:] * scaling + pair_in[...].astype(jnp.float32)).astype(jnp.bfloat16)

    @pl.when(odd == 1)
    def _():
        kvs[...] = (dvk_ref[:, 0:HD] + pair_in[...].astype(jnp.float32)).astype(jnp.bfloat16)

    def kv_cols(sender):
        return pl.ds(pl.multiple_of(lax.rem(sender, 2) * half + sender // 2 * HD, HD), HD)

    def kv_copy(to):
        return pltpu.make_async_remote_copy(
            src_ref=kvs.at[rows_of(to)],
            dst_ref=gkv_ref.at[:, kv_cols(me)],
            send_sem=kv_s.at[to],
            recv_sem=kv_r.at[me],
            device_id={"aa": to},
            device_id_type=MESH,
        )

    def kv_arrival(sender):
        return pltpu.make_async_remote_copy(
            src_ref=kvs.at[rows_of(sender)],
            dst_ref=gkv_ref.at[:, kv_cols(sender)],
            send_sem=kv_s.at[sender],
            recv_sem=kv_r.at[sender],
            device_id={"aa": sender},
            device_id_type=MESH,
        )

    for r in range(1, peers):
        kv_copy(peer(r)).start()
    kv_local = pltpu.make_async_copy(kvs.at[rows_of(me)], gkv_ref.at[:, kv_cols(me)], own_sem.at[3])
    kv_local.start()

    for c in range(chunks):
        gq_local(c).wait()
    kv_local.wait()
    for r in range(1, peers):
        other = peer(r)
        for c in range(chunks):
            gq_arrival(c, other).wait_recv()
        kv_arrival(other).wait_recv()
    for r in range(1, peers):
        other = peer(r)
        for kind in range(4):
            exchange(kind, other, me, r).wait_send()
        for c in range(chunks):
            dout_send(c, other).wait_send()
            gq_copy(c, other).wait_send()
        kv_copy(other).wait_send()
    pair_copy.wait_send()
    for side in range(2):
        for s in range(last):
            @pl.when(gather_sends(side, s))
            def _(side=side, s=s):
                for c in range(chunks):
                    gather(side, c, s).wait_send()


def attention_grads(query, keys, values, segment_ids, grad_out, w_out, scaling):
    peers, planes = lax.axis_size("aa"), lax.axis_size("ba")
    tok = query.shape[0]
    chunks = tok // CHUNK
    total = peers * tok
    blocks = peers * chunks
    low, full = jnp.bfloat16, jnp.float32
    return pl.pallas_call(
        functools.partial(attention_kernel, peers, planes, chunks, scaling),
        out_shape=[
            jax.ShapeDtypeStruct((query.shape[1], tok), low),
            jax.ShapeDtypeStruct((tok, 2 * keys.shape[1]), low),
        ],
        in_specs=[HBM] * 6,
        out_specs=[WHOLE, WHOLE],
        scratch_shapes=[
            pltpu.VMEM(w_out.shape, low),
            pltpu.VMEM((w_out.shape[1], tok), low),
            pltpu.VMEM((total, HD), low),
            pltpu.VMEM((total, HD), low),
            pltpu.VMEM((total, HD), low),
            pltpu.VMEM((HD, total), low),
            pltpu.VMEM((HD, total), low),
            pltpu.VMEM((peers, 1, tok), jnp.int32),
            pltpu.VMEM((peers, 1, tok), full),
            pltpu.VMEM((total, CHUNK), full),
            pltpu.VMEM((blocks * (blocks + 1) // 2 * CHUNK, CHUNK), low),
            pltpu.VMEM((blocks, HD, CHUNK), full),
            pltpu.VMEM((blocks, 1, CHUNK), full),
            pltpu.VMEM((total, 2 * HD), full),
            pltpu.VMEM((chunks, peers, HD, CHUNK), low),
            pltpu.VMEM((chunks, peers, HD, CHUNK), low),
            pltpu.VMEM((chunks, peers, HD, CHUNK), low),
            pltpu.VMEM((total, HD), low),
            pltpu.VMEM((total, HD), low),
            pltpu.VMEM((total, HD), low),
            pltpu.SemaphoreType.DMA,
            pltpu.SemaphoreType.DMA((5,)),
            pltpu.SemaphoreType.DMA((2, chunks, planes - 1)),
            pltpu.SemaphoreType.DMA((2, chunks, planes - 1)),
            pltpu.SemaphoreType.DMA((4, peers)),
            pltpu.SemaphoreType.DMA((4, peers)),
            pltpu.SemaphoreType.DMA((chunks, peers)),
            pltpu.SemaphoreType.DMA((chunks, peers)),
            pltpu.SemaphoreType.DMA((chunks, peers)),
            pltpu.SemaphoreType.DMA((chunks, peers)),
            pltpu.SemaphoreType.DMA,
            pltpu.SemaphoreType.DMA,
            pltpu.SemaphoreType.DMA((peers,)),
            pltpu.SemaphoreType.DMA((peers,)),
        ],
        compiler_params=pltpu.CompilerParams(
            collective_id=0, has_side_effects=True, vmem_limit_bytes=60 * 1024 * 1024
        ),
        name="attention_grads",
    )(query, keys, values, segment_ids.reshape(1, -1), grad_out.T, w_out)


def local(query, keys, values, grad_out, segment_ids, w_query, w_key, w_value, w_out):
    seq_devices, planes = lax.axis_size("aa"), lax.axis_size("ba")
    heads, groups = query.shape[1] // HD, keys.shape[1] // HD
    fits = heads == seq_devices and 2 * groups == heads and planes == 4 and query.shape[0] == 3 * CHUNK
    if not fits:
        return local_ring(query, keys, values, grad_out, segment_ids, w_query, w_key, w_value, w_out)
    scaling = (D / HQ) ** (-0.5)
    grad_q, grad_kv = attention_grads(query, keys, values, segment_ids, grad_out, w_out, scaling)
    return project_scatter(grad_q, grad_kv, w_query, w_key, w_value).T


def solution(mesh):
    return jax.shard_map(
        local,
        mesh=mesh,
        in_specs=(
            P("aa", "ba"),
            P("aa", "ba"),
            P("aa", "ba"),
            P("aa", "ba"),
            P("aa"),
            P(None, "ba"),
            P(None, "ba"),
            P(None, "ba"),
            P("ba", None),
        ),
        out_specs=P("aa", "ba"),
        check_vma=False,
    )
```

time: 273 us -> 233 us (0.85); the launches traced: 275 us -> 232 us
  Pallas kernels: 43.2 us -> 228 us
  waiting for transfers between devices: 125 us -> 0 us
  matrix products: 33.5 us -> 0 us
  blocking collectives: 32.5 us -> 0 us
  starting transfers between devices: 14.9 us -> 0 us
  between operations: 13.6 us -> 0.02 us
  local copies, waits for them, and re-layouts: 8.06 us -> 3.53 us
  other arithmetic: 4.24 us -> 0 us
    pallas_call x2, Pallas kernels: 43.2 us -> 228 us  [the longest x1 137 us: attention_grads(): pl.pallas_call(functools.partial(attention_kernel, peers, planes, chunks,...]
    reduce_scatter x1 -> x0, waiting for transfers between devices: 75.4 us -> none  [local(): lax.psum_scatter(part.astype(jnp.bfloat16), 'ba', scatter_dimension=1, ti...]
    dot_general x4 -> x0, matrix products: 33.5 us -> none  [project_back(): lax.dot_general(grad, weight, (((1,), (1,)), ((), ())), preferred_element...]
    all_gather x1 -> x0, blocking collectives: 32.5 us -> none  [local(): all_seg = lax.all_gather(segment_ids, 'aa', axis=0, tiled=True)]
    all_gather x1 -> x0, waiting for transfers between devices: 24.6 us -> none  [local(): gathered = lax.all_gather(grad_out, 'ba', axis=1, tiled=True)]
    all_to_all x4 -> x0, waiting for transfers between devices: 24.5 us -> none  [exchange(): return lax.all_to_all(value, 'aa', 0, 0, tiled=True)]
    all_to_all x4 -> x0, starting transfers between devices: 14.7 us -> none  [exchange(): return lax.all_to_all(value, 'aa', 0, 0, tiled=True)]
    reshape x5 -> x1, local copies, waits for them, and re-layouts: 5.5 us -> 1.24 us  [attention_grads(): segment_ids.reshape(1, -1)]
  transfers between devices with their start and end apart: 7 -> 0, of which waited for: 5 -> 0; matrix products, arithmetic and copies ran while one was open for 7% -> 0% of each run, Pallas kernels for 5% -> 0%
where the time goes in v1:
time: 233 us; the launch traced here: 232 us
  Pallas kernels  228 us (98%)
  local copies, waits for them, and re-layouts  3.53 us (2%)
    pallas_call x1, Pallas kernels, attention_grads(): pl.pallas_call(functools.partial(attention_kernel, peers, planes, chunks,...  137 us
    pallas_call x1, Pallas kernels, project_scatter(): pl.pallas_call(functools.partial(scatter_kernel, planes), out_shape=jax.S...  90.8 us

profile of v1, /device:TPU:8, one launch (start us, length us, event | category | flops | bytes accessed | tf_op | source)
XLA Modules:
  0.0 231.8 jit_solution(8780062797568759975)
XLA Ops:
  0.0 1.2 reshape.3.seg_ref
  1.2 137.4 %attention_grads.1 = (bf16[1024,384]{1,0:T(8,128)(2,1)}, bf16[384,1024]{1,0:T(8,128)(2,1)}) custom-call(bf16[384,1024]{1,0:T(8,128)(2,1)} %q_ref.1, bf16[384,512]{1,0:T(8,128)(2,1)} %k_ref.1, bf16[384,512]{1,0:T(8,128)(2,1)} %v_ref.1, s32[1,384]{1,0:T(1,128)} %reshape.3.seg_ref, bf16[1344,384]{1,0:T(8,128)(2,1)} %bitcast.3, bf16[1024,5376]{1,0:T(8,128)(2,1)} %w_ref.1), custom_call_target="tpu_custom_call" | custom-call | tf_op jit(solution)/shard_map/attention_grads/pallas_call | solution.py:697
  138.6 90.8 %project_scatter.1 = bf16[1344,384]{1,0:T(8,128)(2,1)} custom-call(bf16[1024,384]{1,0:T(8,128)(2,1)} %get-tuple-element.7.gq_ref, bf16[384,1024]{1,0:T(8,128)(2,1)} %get-tuple-element.8.gkv_ref, bf16[5376,1024]{1,0:T(8,128)(2,1)} %wq_ref.1, bf16[5376,512]{1,0:T(8,128)(2,1)} %wk_ref.1, bf16[5376,512]{1,0:T(8,128)(2,1)} %wv_ref.1), custom_call_target="tpu_custom_call" | custom-call | tf_op jit(solution)/shard_map/project_scatter/pallas_call | solution.py:298
  229.5 2.3 copy.11

commit v2 on v1

--- a/solution.py
+++ b/solution.py
@@ -323,7 +323,7 @@
 
 
 def attention_kernel(peers, planes, chunks, scaling, q_ref, k_ref, v_ref, seg_ref, g_ref, w_ref, gq_ref, gkv_ref,
-                     wbuf, fbuf, qa, ka, va, kt, vt, segs, starts_ref, s_ref, p_ref, ot_ref, inv_ref, dvk_ref,
+                     wbuf, fbuf, qa, ka, va, kt, vt, segs, starts_ref, s_ref, p_ref, ot_ref, inv_ref, dvk_ref, acc_ref,
                      dsend, drecv, gqs, pair_out, pair_in, kvs,
                      local_sem, own_sem, ag_s, ag_r, x_s, x_r, d_s, d_r, gq_s, gq_r, pr_s, pr_r, kv_s, kv_r):
     me = lax.axis_index("aa")
@@ -399,9 +399,9 @@
                     arrival(side, c, s - 1).wait_recv()
                 gather(side, c, s).start()
 
-    def finish_gather(c):
+    def finish_gather(c, steps):
         for side in range(2):
-            for s in range(last):
+            for s in steps:
                 @pl.when((z == last) if side == 0 else (z == 0))
                 def _(side=side, s=s):
                     arrival(side, c, s).wait_recv()
@@ -443,60 +443,61 @@
     relay(0, 2)
     relay(2, 0)
 
-    def tri(m):
-        return m * (m + 1) // 2 * CHUNK
-
-    def stats(c, first):
-        def block(a, carry):
-            m = chunks * a + c
-            if first:
-                @pl.when(a != me)
-                def _():
-                    for kind in range(3):
-                        exchange(kind, me, a, 0).wait_recv()
-
-                kt[:, rows_of(a)] = ka[rows_of(a), :].astype(jnp.float32).T.astype(jnp.bfloat16)
-                vt[:, rows_of(a)] = va[rows_of(a), :].astype(jnp.float32).T.astype(jnp.bfloat16)
-            query = qa[pl.ds(pl.multiple_of(m * CHUNK, CHUNK), CHUNK), :]
-            begin = starts_ref[a, :, c * CHUNK : (c + 1) * CHUNK]
-
-            def scores(at, size, diagonal):
-                span = pl.ds(pl.multiple_of(at, CHUNK), size)
-                s = lax.dot_general(ka[span, :], query, CONTRACT_LAST, preferred_element_type=jnp.float32)
-                key = lax.broadcasted_iota(jnp.int32, (size, CHUNK), 0)
+    def pair_rows(i, at, size):
+        return pl.ds(pl.multiple_of(i * (i + 1) * tok + at, CHUNK), size)
+
+    def stats(start, stop):
+        def block(i, j):
+            a = 2 * i + j
+
+            @pl.when(a != me)
+            def _():
+                for kind in range(3):
+                    exchange(kind, me, a, 0).wait_recv()
+
+            kt[:, rows_of(a)] = ka[rows_of(a), :].astype(jnp.float32).T.astype(jnp.bfloat16)
+            vt[:, rows_of(a)] = va[rows_of(a), :].astype(jnp.float32).T.astype(jnp.bfloat16)
+            query = qa[rows_of(a), :]
+            begin = starts_ref[a]
+
+            def scores(u, diagonal):
+                s = lax.dot_general(ka[rows_of(u), :], query, CONTRACT_LAST, preferred_element_type=jnp.float32)
+                key = lax.broadcasted_iota(jnp.int32, (tok, tok), 0)
+                allowed = (key + u * tok).astype(jnp.float32) >= begin
                 if diagonal:
-                    allowed = key <= c * CHUNK + lax.broadcasted_iota(jnp.int32, (size, CHUNK), 1)
-                    allowed &= (key + at).astype(jnp.float32) >= begin
-                else:
-                    allowed = (key + at).astype(jnp.float32) >= begin
+                    allowed &= key <= lax.broadcasted_iota(jnp.int32, (tok, tok), 1)
                 s = jnp.where(allowed, s * (scaling * LOG2E), NEG_FILL)
-                s_ref[span, :] = s
+                s_ref[rows_of(u), :] = s
                 return fold_rows(s, jnp.max)
 
-            top = lax.fori_loop(0, a, lambda u, t: jnp.maximum(t, scores(u * tok, tok, False)),
-                                jnp.full((8, CHUNK), NEG_FILL, jnp.float32))
-            size = (c + 1) * CHUNK
-            top = jnp.maximum(top, scores(a * tok, size, True))
-            top = jnp.max(top, axis=0, keepdims=True)
-
-            def weights(at, size, state):
+            top = lax.fori_loop(0, a, lambda u, t: jnp.maximum(t, scores(u, False)),
+                                jnp.full((8, tok), NEG_FILL, jnp.float32))
+            top = jnp.max(jnp.maximum(top, scores(a, True)), axis=0, keepdims=True)
+
+            def weights(u, state):
                 total, out = state
-                span = pl.ds(pl.multiple_of(at, CHUNK), size)
-                p = jnp.exp2(s_ref[span, :] - top)
+                p = jnp.exp2(s_ref[rows_of(u), :] - top)
                 low = p.astype(jnp.bfloat16)
-                p_ref[pl.ds(pl.multiple_of(tri(m) + at, CHUNK), size), :] = low
+                for c in range(chunks):
+                    p_ref[c, pair_rows(i, u * tok, tok), j * CHUNK : (j + 1) * CHUNK] = low[:, c * CHUNK : (c + 1) * CHUNK]
                 return (total + fold_rows(p, jnp.sum),
-                        out + jnp.dot(vt[:, span], low, preferred_element_type=jnp.float32))
-
-            state = (jnp.zeros((8, CHUNK), jnp.float32), jnp.zeros((HD, CHUNK), jnp.float32))
-            state = lax.fori_loop(0, a, lambda u, st: weights(u * tok, tok, st), state)
-            total, out = weights(a * tok, size, state)
+                        out + jnp.dot(vt[:, rows_of(u)], low, preferred_element_type=jnp.float32))
+
+            state = (jnp.zeros((8, tok), jnp.float32), jnp.zeros((HD, tok), jnp.float32))
+            total, out = lax.fori_loop(0, a + 1, weights, state)
             inverse = 1.0 / jnp.sum(total, axis=0, keepdims=True)
-            inv_ref[m] = inverse
-            ot_ref[m] = out * inverse
+            inv_ref[a] = inverse
+            ot_ref[a] = out * inverse
+            if j == 0:
+                for c in range(chunks):
+                    p_ref[c, pair_rows(i, (a + 1) * tok, tok), 0:CHUNK] = jnp.zeros((tok, CHUNK), jnp.bfloat16)
+
+        def pair(i, carry):
+            block(i, 0)
+            block(i, 1)
             return carry
 
-        lax.fori_loop(0, peers, block, 0)
+        lax.fori_loop(start, stop, pair, 0)
 
     def dout_send(c, to):
         return pltpu.make_async_remote_copy(
@@ -518,15 +519,24 @@
             device_id_type=MESH,
         )
 
-    def project(c):
-        finish_gather(c)
-        pair = 2
+    depth = planes // 2 * feats
+    near = z // (planes // 2)
+
+    def project_half(c, which):
+        side = near if which == 0 else 1 - near
+        span = pl.ds(pl.multiple_of(side * depth, CHUNK), depth)
+        finish_gather(c, range(1) if which == 0 else range(1, last))
+        group = peers // 2
 
         def heads(i, carry):
-            span = pl.ds(pl.multiple_of(i * (pair * HD), HD), pair * HD)
-            out = jnp.dot(wbuf[span, :], fbuf[:, c * CHUNK : (c + 1) * CHUNK], preferred_element_type=jnp.float32)
-            for j in range(pair):
-                to = i * pair + j
+            rows = pl.ds(pl.multiple_of(i * (group * HD), HD), group * HD)
+            out = jnp.dot(wbuf[rows, span], fbuf[span, c * CHUNK : (c + 1) * CHUNK], preferred_element_type=jnp.float32)
+            if which == 0:
+                acc_ref[c, rows, :] = out
+                return carry
+            out += acc_ref[c, rows, :]
+            for j in range(group):
+                to = i * group + j
                 dsend[c, to] = out[j * HD : (j + 1) * HD, :].astype(jnp.bfloat16)
 
                 @pl.when(to != me)
@@ -535,8 +545,9 @@
 
             return carry
 
-        lax.fori_loop(0, peers // pair, heads, 0)
-        drecv[c, me] = dsend[c, me]
+        lax.fori_loop(0, peers // group, heads, 0)
+        if which == 1:
+            drecv[c, me] = dsend[c, me]
 
     def gq_copy(c, to):
         return pltpu.make_async_remote_copy(
@@ -561,78 +572,114 @@
     def gq_local(c):
         return pltpu.make_async_copy(gqs.at[c, me], gq_ref.at[lanes(me), pl.ds(c * CHUNK, CHUNK)], own_sem.at[c])
 
+    odd = lax.rem(me, 2)
+    partner = me + 1 - 2 * odd
+
+    def pair_span(i):
+        return pl.ds(pl.multiple_of(i * (2 * tok), CHUNK), 2 * tok)
+
+    def pair_copy(i):
+        return pltpu.make_async_remote_copy(
+            src_ref=pair_out.at[pair_span(i)],
+            dst_ref=pair_in.at[pair_span(i)],
+            send_sem=pr_s.at[i],
+            recv_sem=pr_r.at[i],
+            device_id={"aa": partner},
+            device_id_type=MESH,
+        )
+
     def grads(c):
-        def block(a, carry):
-            m = chunks * a + c
-
-            @pl.when(a != me)
-            def _():
-                dout_arrival(c, a).wait_recv()
-
-            query = qa[pl.ds(pl.multiple_of(m * CHUNK, CHUNK), CHUNK), :]
-            dout = (drecv[c, a].astype(jnp.float32) * inv_ref[m]).astype(jnp.bfloat16)
-            delta = jnp.sum(dout.astype(jnp.float32) * ot_ref[m], axis=0, keepdims=True)
-
-            def unit(at, size, grad_q):
-                span = pl.ds(pl.multiple_of(at, CHUNK), size)
-                p = p_ref[pl.ds(pl.multiple_of(tri(m) + at, CHUNK), size), :]
-                dp = jnp.dot(va[span, :], dout, preferred_element_type=jnp.float32)
+        final = c == chunks - 1
+
+        def pair(step, carry):
+            i = peers // 2 - 1 - step
+            douts, queries, deltas = [], [], []
+            for j in range(2):
+                a = 2 * i + j
+
+                @pl.when(a != me)
+                def _():
+                    dout_arrival(c, a).wait_recv()
+
+                cols = slice(c * CHUNK, (c + 1) * CHUNK)
+                dout = (drecv[c, a].astype(jnp.float32) * inv_ref[a, :, cols]).astype(jnp.bfloat16).astype(jnp.float32)
+                deltas.append(jnp.sum(dout * ot_ref[a, :, cols], axis=0, keepdims=True))
+                douts.append(dout)
+                queries.append(qa[pl.ds(pl.multiple_of(a * tok + c * CHUNK, CHUNK), CHUNK), :])
+            dout = jnp.concatenate(douts, axis=1)
+            dout_low = dout.astype(jnp.bfloat16)
+            dout_rows = dout.T.astype(jnp.bfloat16)
+            delta = jnp.concatenate(deltas, axis=1)
+            query = jnp.concatenate(queries, axis=0)
+
+            def unit(u, grad_q):
+                span = pair_span(u)
+                p = p_ref[c, pair_rows(i, u * (2 * tok), 2 * tok), :]
+                dp = jnp.dot(va[span, :], dout_low, preferred_element_type=jnp.float32)
                 ds = (p.astype(jnp.float32) * (dp - delta)).astype(jnp.bfloat16)
-                dvk_ref[span, 0:HD] += lax.dot_general(p, dout, CONTRACT_LAST, preferred_element_type=jnp.float32)
+                dvk_ref[span, 0:HD] += jnp.dot(p, dout_rows, preferred_element_type=jnp.float32)
                 dvk_ref[span, HD:] += jnp.dot(ds, query, preferred_element_type=jnp.float32)
                 return grad_q + jnp.dot(kt[:, span], ds, preferred_element_type=jnp.float32)
 
-            grad_q = lax.fori_loop(0, a, lambda u, t: unit(u * tok, tok, t), jnp.zeros((HD, CHUNK), jnp.float32))
-            grad_q = unit(a * tok, (c + 1) * CHUNK, grad_q)
-            gqs[c, a] = (grad_q * scaling).astype(jnp.bfloat16)
-
-            @pl.when(a != me)
-            def _():
-                gq_copy(c, a).start()
+            grad_q = lax.fori_loop(0, i + 1, unit, jnp.zeros((HD, 2 * CHUNK), jnp.float32))
+            for j in range(2):
+                a = 2 * i + j
+                gqs[c, a] = (grad_q[:, j * CHUNK : (j + 1) * CHUNK] * scaling).astype(jnp.bfloat16)
+
+                @pl.when(a != me)
+                def _():
+                    gq_copy(c, a).start()
+
+            if final:
+                span = pair_span(i)
+
+                @pl.when(odd == 0)
+                def _():
+                    pair_out[span, :] = dvk_ref[span, 0:HD].astype(jnp.bfloat16)
+
+                @pl.when(odd == 1)
+                def _():
+                    pair_out[span, :] = (dvk_ref[span, HD:] * scaling).astype(jnp.bfloat16)
+
+                pair_copy(i).start()
 
             return carry
 
-        lax.fori_loop(0, peers, block, 0)
+        lax.fori_loop(0, peers // 2, pair, 0)
         gq_local(c).start()
 
-    stats(0, True)
+    stats(0, 3)
     relay(1, 2)
-    stats(1, False)
+    stats(3, peers // 2)
     relay(2, 1)
     weight_copy.wait()
-    project(0)
-    stats(2, False)
+    project_half(0, 0)
+    project_half(0, 1)
     relay(2, 2)
-    project(1)
+    project_half(1, 0)
+    project_half(2, 0)
+    project_half(1, 1)
     grads(0)
     grads(1)
-    project(2)
+    project_half(2, 1)
     grads(2)
 
-    odd = lax.rem(me, 2)
-    partner = me + 1 - 2 * odd
-    pair_copy = pltpu.make_async_remote_copy(
-        src_ref=pair_out, dst_ref=pair_in, send_sem=pr_s, recv_sem=pr_r, device_id={"aa": partner}, device_id_type=MESH
-    )
-
-    @pl.when(odd == 0)
-    def _():
-        pair_out[...] = dvk_ref[:, 0:HD].astype(jnp.bfloat16)
-
-    @pl.when(odd == 1)
-    def _():
-        pair_out[...] = (dvk_ref[:, HD:] * scaling).astype(jnp.bfloat16)
-
-    pair_copy.start()
-    pair_copy.wait_recv()
-
-    @pl.when(odd == 0)
-    def _():
-        kvs[...] = (dvk_ref[:, HD:] * scaling + pair_in[...].astype(jnp.float32)).astype(jnp.bfloat16)
-
-    @pl.when(odd == 1)
-    def _():
-        kvs[...] = (dvk_ref[:, 0:HD] + pair_in[...].astype(jnp.float32)).astype(jnp.bfloat16)
+    def join(step, carry):
+        i = peers // 2 - 1 - step
+        span = pair_span(i)
+        pair_copy(i).wait_recv()
+
+        @pl.when(odd == 0)
+        def _():
+            kvs[span, :] = (dvk_ref[span, HD:] * scaling + pair_in[span, :].astype(jnp.float32)).astype(jnp.bfloat16)
+
+        @pl.when(odd == 1)
+        def _():
+            kvs[span, :] = (dvk_ref[span, 0:HD] + pair_in[span, :].astype(jnp.float32)).astype(jnp.bfloat16)
+
+        return carry
+
+    lax.fori_loop(0, peers // 2, join, 0)
 
     def kv_cols(sender):
         return pl.ds(pl.multiple_of(lax.rem(sender, 2) * half + sender // 2 * HD, HD), HD)
@@ -678,7 +725,8 @@
             dout_send(c, other).wait_send()
             gq_copy(c, other).wait_send()
         kv_copy(other).wait_send()
-    pair_copy.wait_send()
+    for i in range(peers // 2):
+        pair_copy(i).wait_send()
     for side in range(2):
         for s in range(last):
             @pl.when(gather_sends(side, s))
@@ -692,7 +740,7 @@
     tok = query.shape[0]
     chunks = tok // CHUNK
     total = peers * tok
-    blocks = peers * chunks
+    pairs = peers // 2
     low, full = jnp.bfloat16, jnp.float32
     return pl.pallas_call(
         functools.partial(attention_kernel, peers, planes, chunks, scaling),
@@ -712,11 +760,12 @@
             pltpu.VMEM((HD, total), low),
             pltpu.VMEM((peers, 1, tok), jnp.int32),
             pltpu.VMEM((peers, 1, tok), full),
-            pltpu.VMEM((total, CHUNK), full),
-            pltpu.VMEM((blocks * (blocks + 1) // 2 * CHUNK, CHUNK), low),
-            pltpu.VMEM((blocks, HD, CHUNK), full),
-            pltpu.VMEM((blocks, 1, CHUNK), full),
+            pltpu.VMEM((total, tok), full),
+            pltpu.VMEM((chunks, pairs * (pairs + 1) * tok, 2 * CHUNK), low),
+            pltpu.VMEM((peers, HD, tok), full),
+            pltpu.VMEM((peers, 1, tok), full),
             pltpu.VMEM((total, 2 * HD), full),
+            pltpu.VMEM((chunks, peers * HD, CHUNK), full),
             pltpu.VMEM((chunks, peers, HD, CHUNK), low),
             pltpu.VMEM((chunks, peers, HD, CHUNK), low),
             pltpu.VMEM((chunks, peers, HD, CHUNK), low),
@@ -733,8 +782,8 @@
             pltpu.SemaphoreType.DMA((chunks, peers)),
             pltpu.SemaphoreType.DMA((chunks, peers)),
             pltpu.SemaphoreType.DMA((chunks, peers)),
-            pltpu.SemaphoreType.DMA,
-            pltpu.SemaphoreType.DMA,
+            pltpu.SemaphoreType.DMA((pairs,)),
+            pltpu.SemaphoreType.DMA((pairs,)),
             pltpu.SemaphoreType.DMA((peers,)),
             pltpu.SemaphoreType.DMA((peers,)),
         ],

time: 233 us -> 195 us (0.84)
  Pallas kernels: 228 us -> 191 us
    pallas_call x1, Pallas kernels: 137 us -> 101 us  [attention_grads(): pl.pallas_call(functools.partial(attention_kernel, peers, planes, chunks,...]
where the time goes in v2:
time: 195 us; the launch traced here: 194 us
  Pallas kernels  191 us (98%)
  local copies, waits for them, and re-layouts  3.53 us (2%)
    pallas_call x1, Pallas kernels, attention_grads(): pl.pallas_call(functools.partial(attention_kernel, peers, planes, chunks,...  101 us
    pallas_call x1, Pallas kernels, project_scatter(): pl.pallas_call(functools.partial(scatter_kernel, planes), out_shape=jax.S...  89.9 us

profile of v2, /device:TPU:8, one launch (start us, length us, event | category | flops | bytes accessed | tf_op | source)
XLA Modules:
  0.0 194.4 jit_solution(18207469948089888239)
XLA Ops:
  0.0 1.2 reshape.3.seg_ref
  1.2 101.0 %attention_grads.1 = (bf16[1024,384]{1,0:T(8,128)(2,1)}, bf16[384,1024]{1,0:T(8,128)(2,1)}) custom-call(bf16[384,1024]{1,0:T(8,128)(2,1)} %q_ref.1, bf16[384,512]{1,0:T(8,128)(2,1)} %k_ref.1, bf16[384,512]{1,0:T(8,128)(2,1)} %v_ref.1, s32[1,384]{1,0:T(1,128)} %reshape.3.seg_ref, bf16[1344,384]{1,0:T(8,128)(2,1)} %bitcast.3, bf16[1024,5376]{1,0:T(8,128)(2,1)} %w_ref.1), custom_call_target="tpu_custom_call" | custom-call | tf_op jit(solution)/shard_map/attention_grads/pallas_call | solution.py:745
  102.2 89.9 %project_scatter.1 = bf16[1344,384]{1,0:T(8,128)(2,1)} custom-call(bf16[1024,384]{1,0:T(8,128)(2,1)} %get-tuple-element.7.gq_ref, bf16[384,1024]{1,0:T(8,128)(2,1)} %get-tuple-element.8.gkv_ref, bf16[5376,1024]{1,0:T(8,128)(2,1)} %wq_ref.1, bf16[5376,512]{1,0:T(8,128)(2,1)} %wk_ref.1, bf16[5376,512]{1,0:T(8,128)(2,1)} %wv_ref.1), custom_call_target="tpu_custom_call" | custom-call | tf_op jit(solution)/shard_map/project_scatter/pallas_call | solution.py:298
  192.1 2.3 %copy.11 = bf16[384,1344]{0,1:T(8,128)(2,1)} copy(bf16[384,1344]{0,1:T(8,128)(2,1)} %bitcast.2) | data formatting | bytes 2064384

commit v3 on v2

--- a/solution.py
+++ b/solution.py
@@ -196,29 +196,26 @@
     sub_rows = rows // SUBS
 
     def target(side, step):
-        return step if side == 0 else last - step
-
-    def sends(side, step):
-        return step < z if side == 0 else step < last - z
-
-    def weight_copies(feature, slot):
+        return jnp.where(side == 0, step, last - step)
+
+    near = jnp.where(2 * z > last, 0, 1)
+    sides = (near, 1 - near)
+    counts = (jnp.maximum(z, last - z), jnp.minimum(z, last - z))
+
+    def weight_copies(feature):
         span = pl.ds(pl.multiple_of(feature * rows, 16), rows)
         return [
-            pltpu.make_async_copy(src.at[span], dst.at[slot], wsem.at[slot, part])
+            pltpu.make_async_copy(src.at[span], dst.at[feature], wsem.at[feature, part])
             for part, (src, dst) in enumerate(((wq_ref, wqb), (wk_ref, wkb), (wv_ref, wvb)))
         ]
 
-    order = [(step, side) for step in range(last) for side in range(2)]
-
-    def slot_of(side, step):
-        return step if side == 0 else last - step
-
-    for step, side in order:
-        @pl.when(sends(side, step))
-        def _(step=step, side=side):
-            for copy in weight_copies(target(side, step), slot_of(side, step)):
-                copy.start()
-    for copy in weight_copies(z, z):
+    for step in range(last):
+        for which in range(2):
+            @pl.when(step < counts[which])
+            def _(step=step, which=which):
+                for copy in weight_copies(target(sides[which], step)):
+                    copy.start()
+    for copy in weight_copies(z):
         copy.start()
 
     pl.semaphore_wait(barrier, jnp.minimum(z, 1) + jnp.minimum(last - z, 1))
@@ -238,34 +235,38 @@
             dst_ref=rbuf.at[side, step, span],
             send_sem=ssem.at[side, step, sub],
             recv_sem=rsem.at[side, step, sub],
-            device_id={"ba": z - 1 if side == 0 else z + 1},
-            device_id_type=MESH,
-        )
-
-    for step, side in order:
-        behind = high if side == 0 else low
-
-        @pl.when(sends(side, step))
-        def _(step=step, side=side, behind=behind):
-            slot = slot_of(side, step)
-            for copy in weight_copies(target(side, step), slot):
-                copy.wait()
-            for sub in range(SUBS):
-                span = pl.ds(sub * sub_rows, sub_rows)
-                acc = part(slot, sub)
-
-                @pl.when(behind)
-                def _():
-                    hop(side, step, sub).wait_recv()
-                    sbuf[side, step, span, :] = (acc + rbuf[side, step, span, :].astype(jnp.float32)).astype(jnp.bfloat16)
-
-                @pl.when(jnp.logical_not(behind))
-                def _():
-                    sbuf[side, step, span, :] = acc.astype(jnp.bfloat16)
-
-                hop(side, step, sub).start()
-
-    for copy in weight_copies(z, z):
+            device_id={"ba": jnp.where(side == 0, z - 1, z + 1)},
+            device_id_type=MESH,
+        )
+
+    inner = low & high
+    order = sorted(
+        [(step * SUBS + sub + 2 * which * (step + 1) - 0.5 * which, which, step, sub)
+         for which in range(2) for step in range(last - which) for sub in range(SUBS)]
+    )
+    for _unused, which, step, sub in order:
+        @pl.when(step < counts[which])
+        def _(which=which, step=step, sub=sub):
+            side = sides[which]
+            feature = target(side, step)
+            if sub == 0:
+                for copy in weight_copies(feature):
+                    copy.wait()
+            span = pl.ds(sub * sub_rows, sub_rows)
+            acc = part(feature, sub)
+
+            @pl.when(inner)
+            def _():
+                hop(side, step, sub).wait_recv()
+                sbuf[side, step, span, :] = (acc + rbuf[side, step, span, :].astype(jnp.float32)).astype(jnp.bfloat16)
+
+            @pl.when(jnp.logical_not(inner))
+            def _():
+                sbuf[side, step, span, :] = acc.astype(jnp.bfloat16)
+
+            hop(side, step, sub).start()
+
+    for copy in weight_copies(z):
         copy.wait()
     for sub in range(SUBS):
         span = pl.ds(sub * sub_rows, sub_rows)
@@ -283,11 +284,12 @@
 
         out_ref[span, :] = total_ref[span, :].astype(jnp.bfloat16)
 
-    for step, side in order:
-        @pl.when(sends(side, step))
-        def _(step=step, side=side):
-            for sub in range(SUBS):
-                hop(side, step, sub).wait_send()
+    for which in range(2):
+        for step in range(last):
+            @pl.when(step < counts[which])
+            def _(which=which, step=step):
+                for sub in range(SUBS):
+                    hop(sides[which], step, sub).wait_send()
 
 
 def project_scatter(gq, gkv, w_query, w_key, w_value):
@@ -325,7 +327,7 @@
 def attention_kernel(peers, planes, chunks, scaling, q_ref, k_ref, v_ref, seg_ref, g_ref, w_ref, gq_ref, gkv_ref,
                      wbuf, fbuf, qa, ka, va, kt, vt, segs, starts_ref, s_ref, p_ref, ot_ref, inv_ref, dvk_ref, acc_ref,
                      dsend, drecv, gqs, pair_out, pair_in, kvs,
-                     local_sem, own_sem, ag_s, ag_r, x_s, x_r, d_s, d_r, gq_s, gq_r, pr_s, pr_r, kv_s, kv_r):
+                     local_sem, own_sem, f_s, ag_s, ag_r, x_s, x_r, d_s, d_r, gq_s, gq_r, pr_s, pr_r, kv_s, kv_r):
     me = lax.axis_index("aa")
     z = lax.axis_index("ba")
     last = planes - 1
@@ -406,6 +408,20 @@
                 def _(side=side, s=s):
                     arrival(side, c, s).wait_recv()
 
+    odd = lax.rem(me, 2)
+    partner = me + 1 - 2 * odd
+
+    def forward(kind, sender, r):
+        land = (ka if kind == 1 else va).at[rows_of(sender)]
+        return pltpu.make_async_remote_copy(
+            src_ref=land,
+            dst_ref=land,
+            send_sem=f_s.at[kind - 1, r],
+            recv_sem=x_r.at[kind, sender],
+            device_id={"aa": partner},
+            device_id_type=MESH,
+        )
+
     def exchange(kind, to, sender, peer_sem):
         shard = (q_ref.at[:, lanes(to)], k_ref.at[:, lanes(to // 2)], v_ref.at[:, lanes(to // 2)], seg_ref)[kind]
         land = (qa.at[rows_of(sender)], ka.at[rows_of(sender)], va.at[rows_of(sender)], segs.at[sender])[kind]
@@ -423,7 +439,10 @@
     for r in range(1, peers):
         exchange(3, peer(r), me, r).start()
     for r in range(1, peers):
-        for kind in range(3):
+        exchange(0, peer(r), me, r).start()
+    for kind in (1, 2):
+        exchange(kind, partner, me, 1).start()
+        for r in range(2, peers, 2):
             exchange(kind, peer(r), me, r).start()
     weight_copy.start()
     dvk_ref[...] = jnp.zeros_like(dvk_ref)
@@ -440,8 +459,10 @@
         before = jnp.sum(jnp.where(ids < doc, 1.0, 0.0), axis=(0, 2), keepdims=True)
         starts = jnp.where(ids == doc, before, starts)
     starts_ref[...] = starts
-    relay(0, 2)
-    relay(2, 0)
+    for kind in (1, 2):
+        for r in range(2, peers, 2):
+            exchange(kind, me, peer(r), r).wait_recv()
+            forward(kind, peer(r), r).start()
 
     def pair_rows(i, at, size):
         return pl.ds(pl.multiple_of(i * (i + 1) * tok + at, CHUNK), size)
@@ -452,7 +473,11 @@
 
             @pl.when(a != me)
             def _():
-                for kind in range(3):
+                exchange(0, me, a, 0).wait_recv()
+
+            @pl.when(lax.rem(a + me, 2) == 1)
+            def _():
+                for kind in (1, 2):
                     exchange(kind, me, a, 0).wait_recv()
 
             kt[:, rows_of(a)] = ka[rows_of(a), :].astype(jnp.float32).T.astype(jnp.bfloat16)
@@ -572,9 +597,6 @@
     def gq_local(c):
         return pltpu.make_async_copy(gqs.at[c, me], gq_ref.at[lanes(me), pl.ds(c * CHUNK, CHUNK)], own_sem.at[c])
 
-    odd = lax.rem(me, 2)
-    partner = me + 1 - 2 * odd
-
     def pair_span(i):
         return pl.ds(pl.multiple_of(i * (2 * tok), CHUNK), 2 * tok)
 
@@ -587,6 +609,46 @@
             device_id={"aa": partner},
             device_id_type=MESH,
         )
+
+    def kv_cols(sender):
+        return pl.ds(pl.multiple_of(lax.rem(sender, 2) * half + sender // 2 * HD, HD), HD)
+
+    def kv_copy(to):
+        return pltpu.make_async_remote_copy(
+            src_ref=kvs.at[rows_of(to)],
+            dst_ref=gkv_ref.at[:, kv_cols(me)],
+            send_sem=kv_s.at[to],
+            recv_sem=kv_r.at[me],
+            device_id={"aa": to},
+            device_id_type=MESH,
+        )
+
+    def kv_arrival(sender):
+        return pltpu.make_async_remote_copy(
+            src_ref=kvs.at[rows_of(sender)],
+            dst_ref=gkv_ref.at[:, kv_cols(sender)],
+            send_sem=kv_s.at[sender],
+            recv_sem=kv_r.at[sender],
+            device_id={"aa": sender},
+            device_id_type=MESH,
+        )
+
+    def join(i):
+        span = pair_span(i)
+        pair_copy(i).wait_recv()
+
+        @pl.when(odd == 0)
+        def _():
+            kvs[span, :] = (dvk_ref[span, HD:] * scaling + pair_in[span, :].astype(jnp.float32)).astype(jnp.bfloat16)
+
+        @pl.when(odd == 1)
+        def _():
+            kvs[span, :] = (dvk_ref[span, 0:HD] + pair_in[span, :].astype(jnp.float32)).astype(jnp.bfloat16)
+
+        for j in range(2):
+            @pl.when(2 * i + j != me)
+            def _():
+                kv_copy(2 * i + j).start()
 
     def grads(c):
         final = c == chunks - 1
@@ -643,12 +705,19 @@
 
                 pair_copy(i).start()
 
+                @pl.when(step > 0)
+                def _():
+                    join(i + 1)
+
             return carry
 
         lax.fori_loop(0, peers // 2, pair, 0)
         gq_local(c).start()
 
-    stats(0, 3)
+    stats(0, 2)
+    relay(0, 2)
+    relay(2, 0)
+    stats(2, 3)
     relay(1, 2)
     stats(3, peers // 2)
     relay(2, 1)
@@ -664,48 +733,7 @@
     project_half(2, 1)
     grads(2)
 
-    def join(step, carry):
-        i = peers // 2 - 1 - step
-        span = pair_span(i)
-        pair_copy(i).wait_recv()
-
-        @pl.when(odd == 0)
-        def _():
-            kvs[span, :] = (dvk_ref[span, HD:] * scaling + pair_in[span, :].astype(jnp.float32)).astype(jnp.bfloat16)
-
-        @pl.when(odd == 1)
-        def _():
-            kvs[span, :] = (dvk_ref[span, 0:HD] + pair_in[span, :].astype(jnp.float32)).astype(jnp.bfloat16)
-
-        return carry
-
-    lax.fori_loop(0, peers // 2, join, 0)
-
-    def kv_cols(sender):
-        return pl.ds(pl.multiple_of(lax.rem(sender, 2) * half + sender // 2 * HD, HD), HD)
-
-    def kv_copy(to):
-        return pltpu.make_async_remote_copy(
-            src_ref=kvs.at[rows_of(to)],
-            dst_ref=gkv_ref.at[:, kv_cols(me)],
-            send_sem=kv_s.at[to],
-            recv_sem=kv_r.at[me],
-            device_id={"aa": to},
-            device_id_type=MESH,
-        )
-
-    def kv_arrival(sender):
-        return pltpu.make_async_remote_copy(
-            src_ref=kvs.at[rows_of(sender)],
-            dst_ref=gkv_ref.at[:, kv_cols(sender)],
-            send_sem=kv_s.at[sender],
-            recv_sem=kv_r.at[sender],
-            device_id={"aa": sender},
-            device_id_type=MESH,
-        )
-
-    for r in range(1, peers):
-        kv_copy(peer(r)).start()
+    join(0)
     kv_local = pltpu.make_async_copy(kvs.at[rows_of(me)], gkv_ref.at[:, kv_cols(me)], own_sem.at[3])
     kv_local.start()
 
@@ -719,12 +747,17 @@
         kv_arrival(other).wait_recv()
     for r in range(1, peers):
         other = peer(r)
-        for kind in range(4):
+        for kind in (0, 3):
             exchange(kind, other, me, r).wait_send()
         for c in range(chunks):
             dout_send(c, other).wait_send()
             gq_copy(c, other).wait_send()
         kv_copy(other).wait_send()
+    for kind in (1, 2):
+        exchange(kind, partner, me, 1).wait_send()
+        for r in range(2, peers, 2):
+            exchange(kind, peer(r), me, r).wait_send()
+            forward(kind, peer(r), r).wait_send()
     for i in range(peers // 2):
         pair_copy(i).wait_send()
     for side in range(2):
@@ -774,6 +807,7 @@
             pltpu.VMEM((total, HD), low),
             pltpu.SemaphoreType.DMA,
             pltpu.SemaphoreType.DMA((5,)),
+            pltpu.SemaphoreType.DMA((2, peers)),
             pltpu.SemaphoreType.DMA((2, chunks, planes - 1)),
             pltpu.SemaphoreType.DMA((2, chunks, planes - 1)),
             pltpu.SemaphoreType.DMA((4, peers)),

time: 195 us -> 177 us (0.908)
  Pallas kernels: 191 us -> 172 us
    pallas_call x1, Pallas kernels: 89.9 us -> 74.1 us  [project_scatter(): pl.pallas_call(functools.partial(scatter_kernel, planes), out_shape=jax.S...]
    pallas_call x1, Pallas kernels: 101 us -> 98 us  [attention_grads(): pl.pallas_call(functools.partial(attention_kernel, peers, planes, chunks,...]
where the time goes in v3:
time: 177 us; the launch traced here: 176 us
  Pallas kernels  172 us (97%)
  local copies, waits for them, and re-layouts  3.53 us (2%)
    pallas_call x1, Pallas kernels, attention_grads(): pl.pallas_call(functools.partial(attention_kernel, peers, planes, chunks,...  98 us
    pallas_call x1, Pallas kernels, project_scatter(): pl.pallas_call(functools.partial(scatter_kernel, planes), out_shape=jax.S...  74.1 us

profile of v3, /device:TPU:8, one launch (start us, length us, event | category | flops | bytes accessed | tf_op | source)
XLA Modules:
  0.0 175.7 jit_solution(13484919162754587219)
XLA Ops:
  0.0 1.2 reshape.3.seg_ref
  1.2 98.0 %attention_grads.1 = (bf16[1024,384]{1,0:T(8,128)(2,1)}, bf16[384,1024]{1,0:T(8,128)(2,1)}) custom-call(bf16[384,1024]{1,0:T(8,128)(2,1)} %q_ref.1, bf16[384,512]{1,0:T(8,128)(2,1)} %k_ref.1, bf16[384,512]{1,0:T(8,128)(2,1)} %v_ref.1, s32[1,384]{1,0:T(1,128)} %reshape.3.seg_ref, bf16[1344,384]{1,0:T(8,128)(2,1)} %bitcast.3, bf16[1024,5376]{1,0:T(8,128)(2,1)} %w_ref.1), custom_call_target="tpu_custom_call" | custom-call | tf_op jit(solution)/shard_map/attention_grads/pallas_call | solution.py:778
  99.3 74.1 %project_scatter.1 = bf16[1344,384]{1,0:T(8,128)(2,1)} custom-call(bf16[1024,384]{1,0:T(8,128)(2,1)} %get-tuple-element.7.gq_ref, bf16[384,1024]{1,0:T(8,128)(2,1)} %get-tuple-element.8.gkv_ref, bf16[5376,1024]{1,0:T(8,128)(2,1)} %wq_ref.1, bf16[5376,512]{1,0:T(8,128)(2,1)} %wk_ref.1, bf16[5376,512]{1,0:T(8,128)(2,1)} %wv_ref.1), custom_call_target="tpu_custom_call" | custom-call | tf_op jit(solution)/shard_map/project_scatter/pallas_call | solution.py:300
  173.4 2.3 %copy.11 = bf16[384,1344]{0,1:T(8,128)(2,1)} copy(bf16[384,1344]{0,1:T(8,128)(2,1)} %bitcast.2) | data formatting | bytes 2064384

commit v4 on v3

--- a/solution.py
+++ b/solution.py
@@ -202,21 +202,36 @@
     sides = (near, 1 - near)
     counts = (jnp.maximum(z, last - z), jnp.minimum(z, last - z))
 
-    def weight_copies(feature):
-        span = pl.ds(pl.multiple_of(feature * rows, 16), rows)
+    def weight_copies(feature, sub):
+        source = pl.ds(pl.multiple_of(feature * rows + sub * sub_rows, 16), sub_rows)
+        span = pl.ds(sub * sub_rows, sub_rows)
         return [
-            pltpu.make_async_copy(src.at[span], dst.at[feature], wsem.at[feature, part])
+            pltpu.make_async_copy(src.at[source], dst.at[feature, span], wsem.at[feature, sub, part])
             for part, (src, dst) in enumerate(((wq_ref, wqb), (wk_ref, wkb), (wv_ref, wvb)))
         ]
 
-    for step in range(last):
-        for which in range(2):
-            @pl.when(step < counts[which])
-            def _(step=step, which=which):
-                for copy in weight_copies(target(sides[which], step)):
-                    copy.start()
-    for copy in weight_copies(z):
-        copy.start()
+    def load(feature, subs):
+        for sub in subs:
+            for copy in weight_copies(feature, sub):
+                copy.start()
+
+    def await_weights(feature, sub):
+        for copy in weight_copies(feature, sub):
+            copy.wait()
+
+    load(target(near, 0), range(1))
+    load(target(near, 0), range(1, SUBS))
+
+    def load_rest():
+        for step in range(last):
+            for which in range(2):
+                if (which, step) == (0, 0):
+                    continue
+
+                @pl.when(step < counts[which])
+                def _(step=step, which=which):
+                    load(target(sides[which], step), range(SUBS))
+        load(z, range(SUBS))
 
     pl.semaphore_wait(barrier, jnp.minimum(z, 1) + jnp.minimum(last - z, 1))
 
@@ -249,9 +264,9 @@
         def _(which=which, step=step, sub=sub):
             side = sides[which]
             feature = target(side, step)
-            if sub == 0:
-                for copy in weight_copies(feature):
-                    copy.wait()
+            await_weights(feature, sub)
+            if (which, step, sub) == (0, 0, 0):
+                load_rest()
             span = pl.ds(sub * sub_rows, sub_rows)
             acc = part(feature, sub)
 
@@ -266,8 +281,8 @@
 
             hop(side, step, sub).start()
 
-    for copy in weight_copies(z):
-        copy.wait()
+    for sub in range(SUBS):
+        await_weights(z, sub)
     for sub in range(SUBS):
         span = pl.ds(sub * sub_rows, sub_rows)
         total_ref[span, :] = part(z, sub)
@@ -309,7 +324,7 @@
             pltpu.VMEM((2, last, rows, tokens), jnp.bfloat16),
             pltpu.VMEM((2, last, rows, tokens), jnp.bfloat16),
             pltpu.VMEM((rows, tokens), jnp.float32),
-            pltpu.SemaphoreType.DMA((planes, 3)),
+            pltpu.SemaphoreType.DMA((planes, SUBS, 3)),
             pltpu.SemaphoreType.DMA((2, last, SUBS)),
             pltpu.SemaphoreType.DMA((2, last, SUBS)),
         ],
@@ -356,12 +371,12 @@
             pltpu.make_async_copy(q_ref.at[:, lanes(me)], qa.at[rows_of(me)], own_sem.at[1]),
             pltpu.make_async_copy(k_ref.at[:, lanes(me // 2)], ka.at[rows_of(me)], own_sem.at[2]),
             pltpu.make_async_copy(v_ref.at[:, lanes(me // 2)], va.at[rows_of(me)], own_sem.at[3]),
-            pltpu.make_async_copy(seg_ref, segs.at[me], own_sem.at[4]),
         ]
 
     weight_copy = pltpu.make_async_copy(w_ref, wbuf, local_sem)
     for copy in own_copies():
         copy.start()
+    segs[me] = seg_ref[...].reshape(1, tok)
     pl.semaphore_wait(barrier, peers + planes - 2)
 
     def gather(side, c, s):
@@ -423,7 +438,7 @@
         )
 
     def exchange(kind, to, sender, peer_sem):
-        shard = (q_ref.at[:, lanes(to)], k_ref.at[:, lanes(to // 2)], v_ref.at[:, lanes(to // 2)], seg_ref)[kind]
+        shard = (q_ref.at[:, lanes(to)], k_ref.at[:, lanes(to // 2)], v_ref.at[:, lanes(to // 2)], segs.at[me])[kind]
         land = (qa.at[rows_of(sender)], ka.at[rows_of(sender)], va.at[rows_of(sender)], segs.at[sender])[kind]
         return pltpu.make_async_remote_copy(
             src_ref=shard,
@@ -781,7 +796,7 @@
             jax.ShapeDtypeStruct((query.shape[1], tok), low),
             jax.ShapeDtypeStruct((tok, 2 * keys.shape[1]), low),
         ],
-        in_specs=[HBM] * 6,
+        in_specs=[HBM, HBM, HBM, WHOLE, HBM, HBM],
         out_specs=[WHOLE, WHOLE],
         scratch_shapes=[
             pltpu.VMEM(w_out.shape, low),
@@ -825,7 +840,7 @@
             collective_id=0, has_side_effects=True, vmem_limit_bytes=60 * 1024 * 1024
         ),
         name="attention_grads",
-    )(query, keys, values, segment_ids.reshape(1, -1), grad_out.T, w_out)
+    )(query, keys, values, segment_ids, grad_out.T, w_out)
 
 
 def local(query, keys, values, grad_out, segment_ids, w_query, w_key, w_value, w_out):

time: 177 us -> 176 us (level)
  no operation moved by 1% of the time
where the time goes in v4:
time: 176 us; the launch traced here: 175 us
  Pallas kernels  172 us (98%)
  local copies, waits for them, and re-layouts  2.28 us (1%)
    pallas_call x1, Pallas kernels, attention_grads(): pl.pallas_call(functools.partial(attention_kernel, peers, planes, chunks,...  98.9 us
    pallas_call x1, Pallas kernels, project_scatter(): pl.pallas_call(functools.partial(scatter_kernel, planes), out_shape=jax.S...  73.6 us

profile of v4, /device:TPU:8, one launch (start us, length us, event | category | flops | bytes accessed | tf_op | source)
XLA Modules:
  0.0 174.8 jit_solution(3884580911939522650)
XLA Ops:
  0.0 98.9 %attention_grads.1 = (bf16[1024,384]{1,0:T(8,128)(2,1)}, bf16[384,1024]{1,0:T(8,128)(2,1)}) custom-call(bf16[384,1024]{1,0:T(8,128)(2,1)} %q_ref.1, bf16[384,512]{1,0:T(8,128)(2,1)} %k_ref.1, bf16[384,512]{1,0:T(8,128)(2,1)} %v_ref.1, s32[384]{0:T(512)} %seg_ref.1, bf16[1344,384]{1,0:T(8,128)(2,1)} %bitcast.3, bf16[1024,5376]{1,0:T(8,128)(2,1)} %w_ref.1), custom_call_target="tpu_custom_call" | custom-call | tf_op jit(solution)/shard_map/attention_grads/pallas_call | solution.py:793
  98.9 73.6 %project_scatter.1 = bf16[1344,384]{1,0:T(8,128)(2,1)} custom-call(bf16[1024,384]{1,0:T(8,128)(2,1)} %get-tuple-element.7.gq_ref, bf16[384,1024]{1,0:T(8,128)(2,1)} %get-tuple-element.8.gkv_ref, bf16[5376,1024]{1,0:T(8,128)(2,1)} %wq_ref.1, bf16[5376,512]{1,0:T(8,128)(2,1)} %wk_ref.1, bf16[5376,512]{1,0:T(8,128)(2,1)} %wv_ref.1), custom_call_target="tpu_custom_call" | custom-call | tf_op jit(solution)/shard_map/project_scatter/pallas_call | solution.py:315
  172.5 2.3 %copy.11 = bf16[384,1344]{0,1:T(8,128)(2,1)} copy(bf16[384,1344]{0,1:T(8,128)(2,1)} %bitcast.2) | data formatting | bytes 2064384
